TPU v7x, 128 devices: a whole 4x4x4 slice. The times are simulated.
128 devices in a mesh: blk: 32 (over y, x_hi, z), hid: 4 (over x_lo, core).
Axes of the slice: x: 4 (x_hi: 2, x_lo: 2; x = x_hi * 2 + x_lo), y: 4, z: 4, core: 2. Of those that a mesh axis runs over, the one named last changes fastest.
Arguments:
- queries: bfloat16 [3072, 128], P('blk'), may hold values from -6 to 6
- node_table: bfloat16 [65536, 128], P('blk'), may hold values from -6 to 6
- beam: int32 [3072, 128], P('blk'), may hold values from 0 to 65535, as said below
- w_query: bfloat16 [128, 256], P(None, 'hid'), may hold values from -0.5 to 0.5
- w_node: bfloat16 [128, 256], P(None, 'hid'), may hold values from -0.5 to 0.5
- w_cross: bfloat16 [128, 256], P(None, 'hid'), may hold values from -0.5 to 0.5
- bias_hidden: bfloat16 [256], P('hid'), may hold values from -3 to 3
- w_out: bfloat16 [256], P('hid'), may hold values from -0.375 to 0.375
Outputs:
- scores: float32 [3072, 128], P('blk', 'hid')
Inputs may be any that keep to these rules, and one draw needn't show every extreme that they name: `beam`: each query's entries are distinct and come in sibling pairs 2p, 2p + 1 of 64 parents. Among the rows of one blk index (96 queries) at most 768 entries lie in any one aligned range of 2048 nodes, and some range holds exactly 768.
All inputs are finite; a program needn't handle non-finite values.
Results may differ from a plain program's by a relative error of at most 0.007.
Values may be sent and summed in bfloat16 or wider, within the bound.
A program may use at most 64 MiB of HBM per device.

v0:
```python
import math

import jax
import jax.numpy as jnp
from jax import lax
from jax.sharding import PartitionSpec as P


def laid_out(blocks, dim):
    blocks = jnp.moveaxis(blocks, 0, dim)
    lengths = blocks.shape
    return blocks.reshape(*lengths[:dim], lengths[dim] * lengths[dim + 1], *lengths[dim + 2 :])


def copy_for_each(value, axis):
    copies = jnp.broadcast_to(value, (lax.axis_size(axis), *value.shape))
    return lax.all_to_all(copies, axis, split_axis=0, concat_axis=0, tiled=True)


def collect(value, axis, dim):
    return laid_out(copy_for_each(value, axis), dim)


def cut_along(value, dim, devices):
    lengths = value.shape
    blocks = value.reshape(*lengths[:dim], devices, lengths[dim] // devices, *lengths[dim + 1 :])
    return jnp.moveaxis(blocks, dim, 0)


def summed_on_arrival(value, axis, dim):
    blocks = cut_along(value, dim, lax.axis_size(axis))
    arrived = lax.all_to_all(blocks, axis, split_axis=0, concat_axis=0, tiled=True)
    return arrived.sum(axis=0)


def select_rows(indices, source_rows):
    onehot = (
        indices[:, None] == jnp.arange(source_rows.shape[0], dtype=jnp.int32)[None, :]
    ).astype(jnp.bfloat16)
    return jnp.dot(onehot, source_rows, preferred_element_type=jnp.float32).astype(jnp.bfloat16)


def shards(queries, node_table, beam, w_query, w_node, w_cross, bias_hidden, w_out):
    query_rows, feat_width = queries.shape
    beam_len = beam.shape[1]
    groups = lax.axis_size("blk")
    shard_rows = node_table.shape[0]
    pair_count = query_rows * beam_len
    capacity = 2 * pair_count // groups
    block_rows = math.gcd(pair_count, 1024)
    block_count = pair_count // block_rows
    flat_ids = beam.reshape(block_count, block_rows)
    owners = flat_ids // shard_rows
    local_plus = flat_ids - owners * shard_rows + 1
    query_plus = (
        jnp.arange(pair_count, dtype=jnp.int32).reshape(block_count, block_rows) // beam_len + 1
    )
    digits = jnp.stack(
        [local_plus // 256, local_plus % 256, query_plus // 256, query_plus % 256], axis=2
    ).astype(jnp.bfloat16)
    lower_mask = (
        jnp.arange(block_rows, dtype=jnp.int32)[:, None]
        > jnp.arange(block_rows, dtype=jnp.int32)[None, :]
    ).astype(jnp.bfloat16)
    group_ids = jnp.arange(groups, dtype=jnp.int32)
    slot_ids = jnp.arange(capacity, dtype=jnp.int32)

    def assign_slots(carry, operands):
        seen_count, slot_table = carry
        block_owner, block_digits = operands
        owner_hot = block_owner[:, None] == group_ids[None, :]
        owner_mask = owner_hot.astype(jnp.bfloat16)
        before = (
            jnp.dot(lower_mask, owner_mask, preferred_element_type=jnp.float32)
            + seen_count[None, :]
        )
        slot_rank = jnp.sum(jnp.where(owner_hot, before, 0.0), axis=1).astype(jnp.int32)
        rank_hot = (slot_rank[:, None] == slot_ids[None, :]).astype(jnp.bfloat16)
        weighted = (owner_mask[:, :, None] * block_digits[:, None, :]).reshape(
            block_rows, groups * 4
        )
        slot_table = slot_table + lax.dot_general(
            weighted, rank_hot, (((0,), (0,)), ((), ())), preferred_element_type=jnp.float32
        )
        seen_count = seen_count + jnp.sum(owner_mask.astype(jnp.float32), axis=0)
        return ((seen_count, slot_table), slot_rank)

    start_carry = (
        jnp.zeros((groups,), jnp.float32),
        jnp.zeros((groups * 4, capacity), jnp.float32),
    )
    (unused_count, slot_table), rank_blocks = lax.scan(assign_slots, start_carry, (owners, digits))
    slot_digits = slot_table.reshape(groups, 4, capacity).astype(jnp.int32)
    requests = slot_digits[:, 0] * 256 + slot_digits[:, 1] - 1
    query_slots = slot_digits[:, 2] * 256 + slot_digits[:, 3] - 1
    stacked_weights = jnp.concatenate([w_query, w_node, w_cross], axis=0)
    bias_row = bias_hidden.astype(jnp.float32)
    out_column = w_out.astype(jnp.float32)

    def score_slots(slot_query, found_rows):
        cross_terms = (slot_query.astype(jnp.float32) * found_rows.astype(jnp.float32)).astype(
            jnp.bfloat16
        )
        joined = jnp.concatenate([slot_query, found_rows, cross_terms], axis=1)
        pre_act = jnp.dot(joined, stacked_weights, preferred_element_type=jnp.float32) + bias_row
        return jnp.dot(jnp.maximum(pre_act, 0.0), out_column, precision=lax.Precision.HIGHEST)

    every_query = collect(queries, "blk", 0)
    query_blocks = every_query.reshape(groups, query_rows, feat_width)
    wanted = lax.all_to_all(requests, "blk", split_axis=0, concat_axis=0, tiled=True)
    asking = lax.all_to_all(query_slots, "blk", split_axis=0, concat_axis=0, tiled=True)

    def one_source(source_parts):
        node_ids, rows_asked, block_queries = source_parts
        return score_slots(
            select_rows(rows_asked, block_queries), select_rows(node_ids, node_table)
        )

    partial_slots = lax.map(one_source, (wanted, asking, query_blocks))
    returned = lax.all_to_all(partial_slots, "blk", split_axis=0, concat_axis=0, tiled=True)
    high_part = returned.astype(jnp.bfloat16)
    remainder = returned - high_part.astype(jnp.float32)
    mid_part = remainder.astype(jnp.bfloat16)
    low_part = (remainder - mid_part.astype(jnp.float32)).astype(jnp.bfloat16)
    stacked_parts = jnp.concatenate([high_part, mid_part, low_part], axis=0)

    def read_block(carry_dummy, operands):
        block_owner, slot_rank = operands
        owner_hot = block_owner[:, None] == group_ids[None, :]
        rank_hot = (slot_rank[:, None] == slot_ids[None, :]).astype(jnp.bfloat16)
        pieces_out = lax.dot_general(
            rank_hot, stacked_parts, (((1,), (1,)), ((), ())), preferred_element_type=jnp.float32
        )
        pieces_out = pieces_out.reshape(block_rows, 3, groups)
        summed = pieces_out[:, 0] + pieces_out[:, 1] + pieces_out[:, 2]
        return (carry_dummy, jnp.sum(jnp.where(owner_hot, summed, 0.0), axis=1))

    carry_dummy, pair_scores = lax.scan(
        read_block, jnp.zeros((), jnp.float32), (owners, rank_blocks)
    )
    partial_scores = pair_scores.reshape(query_rows, beam_len)
    return summed_on_arrival(partial_scores, "hid", 1)


def solution(mesh):
    in_specs = (
        P("blk", None),
        P("blk", None),
        P("blk", None),
        P(None, "hid"),
        P(None, "hid"),
        P(None, "hid"),
        P("hid"),
        P("hid"),
    )
    out_specs = P("blk", "hid")
    return jax.shard_map(shards, mesh=mesh, in_specs=in_specs, out_specs=out_specs, check_vma=False)
```

profile of v0, /device:TPU:1, one launch (start us, length us, event | category | flops | bytes accessed | tf_op | source)
XLA Modules:
  0.0 196.3 jit_solution(41761095201214844)
XLA Ops:
  1.1 1.3 fusion.59
  3.0 23.4 %while.41 = (s32[]{:T(128)}, f32[32]{0:T(128)S(1)}, f32[128,768]{1,0:T(8,128)S(1)}, s32[12,1024]{1,0:T(8,128)S(1)}, s32[12,1024]{1,0:T(8,128)S(1)}, /*index=5*/bf16[12,1024,4]{1,2,0:T(4,128)(2,1)S(1)}) while((s32[]{:T(128)}, f32[32]{0:T(128)S(1)}, f32[128,768]{1,0:T(8,128)S(1)}, s32[12,1024]{1,0:T(8,128)S(1)}, ...), condition=%wide.region_3.4_spmd.clone.clone, body=%wide.region_0.3_spmd.clone.sunk.clone | while | flops 272007200 | bytes 2036572 | solution.py:92
  4.0 0.9 fusion.117
  5.9 0.8 fusion.117
  7.9 0.8 fusion.117
  9.8 0.8 fusion.117
  26.9 20.1 %all_to_all.40 = s32[32,1,768]{2,1,0:T(1,128)S(1)} all-to-all(s32[32,1,768]{2,1,0:T(1,128)S(1)} %get-tuple-element.231), channel_id=1, replica_groups=mesh['blk'=32,'hid'=4] {'blk'}, dimensions={0} | all-to-all | bytes 196608 | tf_op jit(solution)/shard_map/all_to_all | solution.py:110
  47.0 12.4 %all_to_all.41 = s32[32,1,768]{2,1,0:T(1,128)S(1)} all-to-all(s32[32,1,768]{2,1,0:T(1,128)S(1)} %get-tuple-element.232), channel_id=1, replica_groups=mesh['blk'=32,'hid'=4] {'blk'}, dimensions={0} | all-to-all | bytes 196608 | tf_op jit(solution)/shard_map/all_to_all | solution.py:111
  59.4 1.0 broadcast_in_dim.42
  60.4 4.1 %all-to-all-start.1 = ((bf16[32,96,128]{2,1,0:T(8,128)(2,1)}), bf16[32,96,128]{2,1,0:T(8,128)(2,1)S(1)}, u32[]{:S(2)}, u32[]{:S(2)}) async-start(bf16[32,96,128]{2,1,0:T(8,128)(2,1)} %broadcast_in_dim.42), calls=%async_computation.1 | async-start | bytes 1572864 | tf_op jit(solution)/shard_map/all_to_all | solution.py:17
  64.9 12.1 %all-to-all-done.1 = bf16[32,96,128]{2,1,0:T(8,128)(2,1)S(1)} async-done(((bf16[32,96,128]{2,1,0:T(8,128)(2,1)}), bf16[32,96,128]{2,1,0:T(8,128)(2,1)S(1)}, u32[]{:S(2)}, u32[]{:S(2)}) %all-to-all-start.1) | async-done | bytes 786464 | tf_op jit(solution)/shard_map/all_to_all | solution.py:17
  77.0 81.6 %while.39 = (s32[]{:T(128)}, f32[32,768]{1,0:T(8,128)S(1)}, s32[32,768]{1,0:T(8,128)S(1)}, bf16[32,96,128]{2,1,0:T(8,128)(2,1)S(1)}, s32[32,768]{1,0:T(8,128)S(1...) while((s32[]{:T(128)}, f32[32,768]{1,0:T(8,128)S(1)}, ...), condition=%wide.region_5.6_spmd.clone, body=%wide.region_4.5_spmd.sunk.clone | while | flops 463970304 | bytes 2396777 | solution.py:119
  77.4 1.6 multiply_convert_fusion.3
  80.0 1.6 multiply_convert_fusion.3
  82.5 1.6 multiply_convert_fusion.3
  85.1 1.6 multiply_convert_fusion.3
  87.6 1.6 multiply_convert_fusion.3
  90.2 1.6 multiply_convert_fusion.3
  92.7 1.6 multiply_convert_fusion.3
  95.3 1.6 multiply_convert_fusion.3
  97.8 1.6 multiply_convert_fusion.3
  100.4 1.6 multiply_convert_fusion.3
  102.9 1.6 multiply_convert_fusion.3
  105.5 1.6 multiply_convert_fusion.3
  108.0 1.6 multiply_convert_fusion.3
  110.6 1.6 multiply_convert_fusion.3
  113.1 1.6 multiply_convert_fusion.3
  115.7 1.6 multiply_convert_fusion.3
  118.2 1.6 multiply_convert_fusion.3
  120.8 1.6 multiply_convert_fusion.3
  123.3 1.6 multiply_convert_fusion.3
  125.9 1.6 multiply_convert_fusion.3
  128.4 1.6 multiply_convert_fusion.3
  131.0 1.6 multiply_convert_fusion.3
  133.5 1.6 multiply_convert_fusion.3
  136.1 1.6 multiply_convert_fusion.3
  138.6 1.6 multiply_convert_fusion.3
  141.2 1.6 multiply_convert_fusion.3
  143.7 1.6 multiply_convert_fusion.3
  146.3 1.6 multiply_convert_fusion.3
  148.9 1.6 multiply_convert_fusion.3
  151.4 1.6 multiply_convert_fusion.3
  154.0 1.6 multiply_convert_fusion.3
  156.5 1.6 multiply_convert_fusion.3
  159.4 3.9 %all-to-all-start.3 = ((f32[32,1,768]{2,1,0:T(1,128)}), f32[32,1,768]{2,1,0:T(1,128)S(1)}, u32[]{:S(2)}, u32[]{:S(2)}) async-start(f32[32,1,768]{2,1,0:T(1,128)} %all_to_all.31), calls=%async_computation.3 | async-start | bytes 196608 | tf_op jit(solution)/shard_map/all_to_all | solution.py:120
  163.2 8.9 %all-to-all-done.3 = f32[32,1,768]{2,1,0:T(1,128)S(1)} async-done(((f32[32,1,768]{2,1,0:T(1,128)}), f32[32,1,768]{2,1,0:T(1,128)S(1)}, u32[]{:S(2)}, u32[]{:S(2)}) %all-to-all-start.3) | async-done | bytes 98336 | tf_op jit(solution)/shard_map/all_to_all | solution.py:120
  172.2 12.0 %while.40 = (s32[]{:T(128)}, f32[12,1024]{1,0:T(8,128)S(1)}, s32[12,1024]{1,0:T(8,128)S(1)}, s32[12,1024]{1,0:T(8,128)S(1)}, bf16[96,768]{1,0:T(8,128)(2,1)S(1)}) while((s32[]{:T(128)}, f32[12,1024]{1,0:T(8,128)S(1)}, s32[12,1024]{1,0:T(8,128)S(1)}, s32[12,1024]{1,0:T(8,128)S(1)}, bf16[96,768]{1,0:T(8,128)(2,1)S(1)}) %tuple.89), condition=%wide.region_8.9_spmd.clone.clone, body=%wide.region_6.8_spmd.clone.sunk.clone | while | flops 151944192 | bytes 970821 | solution.py:138
  184.5 11.2 %all_to_all.42 = f32[4,96,32]{1,2,0:T(8,128)S(1)} all-to-all(f32[4,96,32]{1,2,0:T(8,128)S(1)} %copy.27), channel_id=1, replica_groups=mesh['blk'=32,'hid'=4] {'hid'}, dimensions={0} | all-to-all | bytes 98304 | tf_op jit(solution)/shard_map/all_to_all | solution.py:32
  (378 shorter events, 64.5 us)
Async XLA Ops:
  26.5 32.9 %copy-start = (bf16[96,128]{1,0:T(8,128)(2,1)S(1)}, bf16[96,128]{1,0:T(8,128)(2,1)}, u32[]{:S(2)}) copy-start(bf16[96,128]{1,0:T(8,128)(2,1)} %param.14) | copy-start | bytes 73732
  60.4 4.1 %copy-start.1 = (bf16[128,64]{0,1:T(8,128)(2,1)S(1)}, bf16[128,64]{0,1:T(8,128)(2,1)}, u32[]{:S(2)}) copy-start(bf16[128,64]{0,1:T(8,128)(2,1)} %param.17) | copy-start | bytes 49156
  60.4 4.2 %copy-start.2 = (bf16[128,64]{0,1:T(8,128)(2,1)S(1)}, bf16[128,64]{0,1:T(8,128)(2,1)}, u32[]{:S(2)}) copy-start(bf16[128,64]{0,1:T(8,128)(2,1)} %param.18) | copy-start | bytes 49156
  60.4 4.4 %copy-start.3 = (bf16[128,64]{0,1:T(8,128)(2,1)S(1)}, bf16[128,64]{0,1:T(8,128)(2,1)}, u32[]{:S(2)}) copy-start(bf16[128,64]{0,1:T(8,128)(2,1)} %param.19) | copy-start | bytes 49156
  60.4 4.5 %copy-start.5 = (bf16[64]{0:T(256)(128)(2,1)S(1)}, bf16[64]{0:T(256)(128)(2,1)}, u32[]{:S(2)}) copy-start(bf16[64]{0:T(256)(128)(2,1)} %param.20) | copy-start | bytes 388
  60.4 4.5 %copy-start.6 = (bf16[64]{0:T(256)(128)(2,1)S(1)}, bf16[64]{0:T(256)(128)(2,1)}, u32[]{:S(2)}) copy-start(bf16[64]{0:T(256)(128)(2,1)} %param.21) | copy-start | bytes 388
  60.4 16.6 %copy-start.4 = (bf16[2048,128]{1,0:T(8,128)(2,1)S(1)}, bf16[2048,128]{1,0:T(8,128)(2,1)}, u32[]{:S(2)}) copy-start(bf16[2048,128]{1,0:T(8,128)(2,1)} %param.15) | copy-start | bytes 1572868
  60.4 16.6 %all-to-all-start.1 = ((bf16[32,96,128]{2,1,0:T(8,128)(2,1)}), bf16[32,96,128]{2,1,0:T(8,128)(2,1)S(1)}, u32[]{:S(2)}, u32[]{:S(2)}) async-start(bf16[32,96,128]{2,1,0:T(8,128)(2,1)} %broadcast_in_dim.42), calls=%async_computation.1 | async-start | bytes 1572864 | tf_op jit(solution)/shard_map/all_to_all | solution.py:17
  159.4 12.8 %all-to-all-start.3 = ((f32[32,1,768]{2,1,0:T(1,128)}), f32[32,1,768]{2,1,0:T(1,128)S(1)}, u32[]{:S(2)}, u32[]{:S(2)}) async-start(f32[32,1,768]{2,1,0:T(1,128)} %all_to_all.31), calls=%async_computation.3 | async-start | bytes 196608 | tf_op jit(solution)/shard_map/all_to_all | solution.py:120
where the time goes:
time: 197 us; the launch traced here: 196 us
  matrix products  102 us (52%)
  blocking collectives  43.6 us (22%)
  waiting for transfers between devices  21 us (11%)
  local copies, waits for them, and re-layouts  10.8 us (5%)
  starting transfers between devices  7.91 us (4%)
  other arithmetic  7.23 us (4%)
  loops' own time  3.42 us (2%)
    dot_general x64, matrix products, select_rows(): jnp.dot(onehot, source_rows, preferred_element_type=jnp.float32)  60.8 us
    all_to_all x1, blocking collectives, shards(): lax.all_to_all(requests, 'blk', split_axis=0, concat_axis=0, tiled=True)  20.1 us
    all_to_all x1, blocking collectives, shards(): lax.all_to_all(query_slots, 'blk', split_axis=0, concat_axis=0, tiled=True)  12.4 us
    all_to_all x1, waiting for transfers between devices, copy_for_each(): return lax.all_to_all(copies, axis, split_axis=0, concat_axis=0, tiled=True)  12.1 us
    all_to_all x1, blocking collectives, summed_on_arrival(): lax.all_to_all(blocks, axis, split_axis=0, concat_axis=0, tiled=True)  11.2 us
    dot_general x12, matrix products, assign_slots(): lax.dot_general(weighted, rank_hot, (((0,), (0,)), ((), ())), preferred_e...  10.2 us
    dot_general x12, matrix products, read_block(): lax.dot_general(rank_hot, stacked_parts, (((1,), (1,)), ((), ())), prefer...  9.55 us
    all_to_all x1, waiting for transfers between devices, shards(): lax.all_to_all(partial_slots, 'blk', split_axis=0, concat_axis=0, tiled=T...  8.94 us
  transfers between devices with their start and end apart: 2, of which 2 were waited for; matrix products, arithmetic and copies ran while one was open for 0% of the time, Pallas kernels for 0%

commit v1 on v0

v1 whole, which is shorter than its diff:
```python
import functools

import jax
import jax.numpy as jnp
from jax import lax
from jax.experimental import pallas as pl
from jax.experimental.pallas import tpu as pltpu
from jax.sharding import PartitionSpec as P

BF16, F32, I32 = jnp.bfloat16, jnp.float32, jnp.int32
GROUPS = 32
SHARES = 4
SERVED = GROUPS // SHARES
Q = 96
BEAM = 128
D = 128
HID = 256
HID_DEV = HID // SHARES
PARENTS = 1024
ROWS = 3
SLOTS = ROWS * 128
COLS = BEAM // SHARES
Q4 = Q // 4
MESH = pl.DeviceIdType.MESH


def nt(a, b):
    return lax.dot_general(a, b, (((1,), (1,)), ((), ())), preferred_element_type=F32)


def nn(a, b):
    return jnp.dot(a, b, preferred_element_type=F32)


def iota(shape, dim):
    return lax.broadcasted_iota(I32, shape, dim)


def flag(cond):
    return jnp.where(cond, 1.0, 0.0).astype(BF16)


def eye(n):
    return flag(iota((n, n), 0) == iota((n, n), 1))


def base_counts(group, even):
    lower = flag(iota((Q, Q), 0) > iota((Q, Q), 1))
    ones = jnp.ones((BEAM, BEAM), BF16)
    masks = [flag((group == i) & even) for i in range(SERVED)]
    before = nn(lower, jnp.concatenate(masks, axis=1)).astype(BF16)
    tall = jnp.concatenate([before[:, i * BEAM : (i + 1) * BEAM] for i in range(SERVED)], axis=0)
    total = nn(tall, ones)
    picked = jnp.zeros((Q, BEAM), F32)
    for i in range(SERVED):
        picked = jnp.where(group == i, total[i * Q : (i + 1) * Q], picked)
    return picked.astype(I32)


def kernel(
    q_ref, table_ref, beam_ref, wq_ref, wn_ref, wc_ref, vec_ref, out_ref,
    w_all, qbuf, req, reqbuf, ret, retbuf, tt, t32, inner, code_s, jl_s, a_s, b_s, wo_s, bi_s, code4, jl4, out4,
    q_send, q_recv, r_send, r_recv, w_send, w_recv, s_send, s_recv,
):
    b, h = lax.axis_index("blk"), lax.axis_index("hid")
    y, xh, z = b // 8, (b // 4) % 2, b % 4
    xl, core = h // 2, h % 2
    my_server = (y % 2) * 2 + z % 2
    my_place = (y // 2) * 4 + xh * 2 + z // 2
    own_xh = (xh + xl + y) % 2
    own_zl = 1 - core

    def owner_of(i):
        return (i // 2) * 8 + own_xh * 4 + (i % 2) * 2 + own_zl

    def source_of(k):
        return ((k // 4) * 2 + xl) * 8 + ((k // 2) % 2) * 4 + (k % 2) * 2 + core

    barrier = pltpu.get_barrier_semaphore()
    served_self = my_server == h

    @pl.loop(0, GROUPS)
    def _(o):
        @pl.when(jnp.logical_not(served_self & (o == b)))
        def _():
            pl.semaphore_signal(barrier, inc=1, device_id={"blk": o, "hid": my_server}, device_id_type=MESH)

    @pl.loop(0, SERVED)
    def _(k):
        for d in range(SHARES):
            @pl.when(jnp.logical_not((d == h) & (source_of(k) == b)))
            def _():
                pl.semaphore_signal(barrier, inc=1, device_id={"blk": source_of(k), "hid": d}, device_id_type=MESH)

    for d in range(1, SHARES):
        pl.semaphore_signal(barrier, inc=1, device_id={"blk": b, "hid": (h + d) % SHARES}, device_id_type=MESH)

    ident = eye(HID_DEV)
    vectors = jnp.concatenate(
        [jnp.broadcast_to(vec_ref[0:1, :], (64, HID_DEV)), jnp.broadcast_to(vec_ref[1:2, :], (64, HID_DEV))], axis=0
    ).astype(BF16)
    mine = jnp.concatenate(
        [nt(ident, wn_ref[...]), nt(ident, wc_ref[...]), nt(ident, wq_ref[...]), nt(ident, vectors)], axis=1
    ).astype(BF16)
    my_rows = pl.ds(pl.multiple_of(h * HID_DEV, HID_DEV), HID_DEV)
    w_all[my_rows, :] = mine

    beam = beam_ref[...]
    even = (beam & 1) == 0
    parent = beam >> 1
    owner = beam >> 11
    local = parent & (PARENTS - 1)
    keys = jnp.where(even, parent, 1 << 20)

    def count(t, acc):
        gap = parent - pltpu.roll(keys, t, 1)
        return acc + jnp.where((gap > 0) & (gap <= local), 1, 0)

    within = lax.fori_loop(1, BEAM, count, jnp.zeros((Q, BEAM), I32), unroll=False)
    inner[...] = within

    asked = ((owner >> 2) & 1 == own_xh) & ((owner & 1) == own_zl)
    group = jnp.where(asked, (owner >> 3) * 2 + ((owner >> 1) & 1), 64)
    rank = within + base_counts(group, even)
    code_s[...] = jnp.where(even, group * 4 + (rank >> 7), 999)
    jl_s[...] = rank & 127
    a_s[...] = (local & 255).astype(F32)
    b_s[...] = (iota((Q, BEAM), 0) + 96 * (local >> 8) - 192).astype(F32)

    pl.semaphore_wait(barrier, 2 * GROUPS + SHARES - 1 - jnp.where(served_self, 2, 0))

    def q_copy(i):
        return pltpu.make_async_remote_copy(
            src_ref=q_ref, dst_ref=qbuf.at[my_place], send_sem=q_send.at[i], recv_sem=q_recv.at[my_place],
            device_id={"blk": owner_of(i), "hid": my_server}, device_id_type=MESH,
        )

    def r_copy(i):
        return pltpu.make_async_remote_copy(
            src_ref=req.at[i], dst_ref=reqbuf.at[my_place], send_sem=r_send.at[i], recv_sem=r_recv.at[my_place],
            device_id={"blk": owner_of(i), "hid": my_server}, device_id_type=MESH,
        )

    def w_copy(d):
        return pltpu.make_async_remote_copy(
            src_ref=w_all.at[my_rows], dst_ref=w_all.at[my_rows], send_sem=w_send.at[d - 1], recv_sem=w_recv.at[d - 1],
            device_id={"blk": b, "hid": (h + d) % SHARES}, device_id_type=MESH,
        )

    @pl.loop(0, SERVED)
    def _(i):
        q_copy(i).start()

    row64 = iota((64, BEAM), 0)
    target = (row64 >> 3) * 4 + (row64 & 3)
    first_part = (row64 & 4) == 0
    lane_id = iota((BEAM, BEAM), 0)

    def compact(step, acc):
        values, places = [], []
        for u in range(2):
            at = pl.ds(2 * step + u, 1)
            payload = jnp.where(first_part, a_s[at, :], b_s[at, :])
            values.append(jnp.where(code_s[at, :] == target, payload, 0.0))
            places.append(jnp.where(lane_id == jl_s[at, :], 1.0, 0.0))
        return acc + nt(jnp.concatenate(values, axis=1).astype(BF16), jnp.concatenate(places, axis=1).astype(BF16))

    tables = lax.fori_loop(0, Q // 2, compact, jnp.zeros((64, BEAM), F32), unroll=False)
    for i in range(SERVED):
        req[i] = tables[8 * i : 8 * i + 8]

    @pl.loop(0, SERVED)
    def _(i):
        r_copy(i).start()

    for d in range(1, SHARES):
        w_copy(d).start()

    t32[...] = table_ref[...].astype(F32)
    ident = eye(D)
    for child in range(2):
        half = t32[pl.ds(child, PARENTS, stride=2), :].astype(BF16)
        tt[child * D : (child + 1) * D, :] = nt(ident, half).astype(BF16)

    def all_owners(g, acc):
        return acc + base_counts(owner - g * SERVED, even)

    rank = lax.fori_loop(0, GROUPS // SERVED, all_owners, inner[...], unroll=False)
    code = owner * 8 + (beam & 1) * 4 + (rank >> 7)
    lane, column = iota((BEAM, 4 * BEAM), 0), iota((BEAM, 4 * BEAM), 1)
    fold, column = column >> 7, column & 127
    select = flag(((column >> 5) == fold) & (lane == h * COLS + (column & 31)))
    for values, place in ((code, code4), (rank & 127, jl4)):
        wide = nn(values.astype(F32).astype(BF16), select)
        folded = jnp.zeros((Q4, BEAM), F32)
        for f in range(4):
            folded = folded + wide[f * Q4 : (f + 1) * Q4, f * BEAM : (f + 1) * BEAM]
        place[...] = folded.astype(I32)

    for d in range(1, SHARES):
        w_copy(d).wait_recv()
    bi_s[...] = jnp.broadcast_to(w_all[:, 3 * D : 3 * D + 1].astype(F32), (HID, 128))
    wo_s[...] = jnp.broadcast_to(w_all[:, 3 * D + 64 : 3 * D + 65].astype(F32), (HID, 128))

    def s_copy(k, d):
        return pltpu.make_async_remote_copy(
            src_ref=ret.at[k], dst_ref=retbuf.at[b], send_sem=s_send.at[k * SHARES + d], recv_sem=s_recv.at[b],
            device_id={"blk": source_of(k), "hid": d}, device_id_type=MESH,
        )

    @pl.loop(0, SERVED)
    def _(k):
        pltpu.make_async_remote_copy(
            src_ref=q_ref, dst_ref=qbuf.at[k], send_sem=q_send.at[k], recv_sem=q_recv.at[k],
            device_id={"blk": source_of(k), "hid": (h + 1) % SHARES}, device_id_type=MESH,
        ).wait_recv()
        pltpu.make_async_remote_copy(
            src_ref=req.at[k], dst_ref=reqbuf.at[k], send_sem=r_send.at[k], recv_sem=r_recv.at[k],
            device_id={"blk": source_of(k), "hid": (h + 1) % SHARES}, device_id_type=MESH,
        ).wait_recv()
        digits = reqbuf[k]
        low, rest = digits[0:4], digits[4:8] + 192.0
        high = jnp.where(rest >= 96.0, 1.0, 0.0) + jnp.where(rest >= 192.0, 1.0, 0.0) + jnp.where(rest >= 288.0, 1.0, 0.0)
        asking = (rest - 96.0 * high).astype(I32)
        wanted = (low + 256.0 * high).astype(I32)
        asking = jnp.concatenate([asking[r : r + 1] for r in range(ROWS)], axis=1)
        wanted = jnp.concatenate([wanted[r : r + 1] for r in range(ROWS)], axis=1)
        found = jnp.zeros((2 * D, SLOTS), F32)
        for c in range(PARENTS // 256):
            hot = flag(iota((256, SLOTS), 0) == wanted - 256 * c)
            found = found + nn(tt[:, c * 256 : (c + 1) * 256], hot)
        hot = flag(iota((Q, SLOTS), 0) == asking)
        query = nn(nt(eye(D), qbuf[k]).astype(BF16), hot)
        bias = jnp.concatenate([bi_s[...]] * ROWS, axis=1)
        weight = jnp.concatenate([wo_s[...]] * ROWS, axis=1)
        shared = nn(w_all[:, 2 * D : 3 * D], query.astype(BF16)) + bias
        rows = []
        for child in range(2):
            node = found[child * D : (child + 1) * D]
            joined = jnp.concatenate([node.astype(BF16), (node * query).astype(BF16)], axis=0)
            hidden = jnp.maximum(nn(w_all[:, : 2 * D], joined) + shared, 0.0)
            score = jnp.sum(hidden * weight, axis=0, keepdims=True)
            rows += [score[:, r * 128 : (r + 1) * 128] for r in range(ROWS)] + [jnp.zeros((1, 128), F32)]
        scores = jnp.concatenate(rows, axis=0)
        ret[k] = scores
        for d in range(SHARES):
            here = (d == h) & (source_of(k) == b)

            @pl.when(here)
            def _():
                retbuf[b] = scores

            @pl.when(jnp.logical_not(here))
            def _():
                s_copy(k, d).start()

    @pl.loop(0, GROUPS)
    def _(o):
        @pl.when(jnp.logical_not(served_self & (o == b)))
        def _():
            pltpu.make_async_remote_copy(
                src_ref=ret.at[0], dst_ref=retbuf.at[o], send_sem=s_send.at[0], recv_sem=s_recv.at[o],
                device_id={"blk": b, "hid": (h + 1) % SHARES}, device_id_type=MESH,
            ).wait_recv()

    table = retbuf[...].reshape(GROUPS * 8, 128)
    coarse = table.astype(BF16)
    fine = (table - coarse.astype(F32)).astype(BF16)
    slot_row = iota((GROUPS * 8, 2 * 128), 0)

    def read(step, carry):
        r0, r1 = pl.ds(2 * step, 1), pl.ds(2 * step + 1, 1)
        place = jnp.concatenate([jl4[r0, :], jl4[r1, :]], axis=1)
        which = jnp.concatenate([code4[r0, :], code4[r1, :]], axis=1)
        hot = flag(iota((128, 2 * 128), 0) == place)
        seen = nn(coarse, hot) + nn(fine, hot)
        score = jnp.sum(jnp.where(slot_row == which, seen, 0.0), axis=0, keepdims=True)
        out4[r0, :] = score[:, :128]
        out4[r1, :] = score[:, 128:]
        return carry

    lax.fori_loop(0, Q4 // 2, read, 0, unroll=False)
    for f in range(4):
        out_ref[f * Q4 : (f + 1) * Q4, :] = out4[:, f * COLS : (f + 1) * COLS]

    @pl.loop(0, SERVED)
    def _(i):
        q_copy(i).wait_send()
        r_copy(i).wait_send()
        for d in range(SHARES):
            @pl.when(jnp.logical_not((d == h) & (source_of(i) == b)))
            def _():
                s_copy(i, d).wait_send()

    for d in range(1, SHARES):
        w_copy(d).wait_send()


def shards(queries, node_table, beam, w_query, w_node, w_cross, bias_hidden, w_out):
    vectors = jnp.stack([bias_hidden, w_out]).astype(F32)
    dma = pltpu.SemaphoreType.DMA
    return pl.pallas_call(
        kernel,
        out_shape=jax.ShapeDtypeStruct((Q, COLS), F32),
        in_specs=[pl.BlockSpec(memory_space=pltpu.VMEM)] * 7,
        out_specs=pl.BlockSpec(memory_space=pltpu.VMEM),
        scratch_shapes=[
            pltpu.VMEM((HID, 4 * D), BF16),
            pltpu.VMEM((SERVED, Q, D), BF16),
            pltpu.VMEM((SERVED, 8, 128), F32),
            pltpu.VMEM((SERVED, 8, 128), F32),
            pltpu.VMEM((SERVED, 8, 128), F32),
            pltpu.VMEM((GROUPS, 8, 128), F32),
            pltpu.VMEM((2 * D, PARENTS), BF16),
            pltpu.VMEM((2 * PARENTS, D), F32),
            pltpu.VMEM((Q, BEAM), I32),
            pltpu.VMEM((Q, BEAM), I32),
            pltpu.VMEM((Q, BEAM), I32),
            pltpu.VMEM((Q, BEAM), F32),
            pltpu.VMEM((Q, BEAM), F32),
            pltpu.VMEM((HID, 128), F32),
            pltpu.VMEM((HID, 128), F32),
            pltpu.VMEM((Q4, 128), I32),
            pltpu.VMEM((Q4, 128), I32),
            pltpu.VMEM((Q4, 128), F32),
            dma((SERVED,)), dma((SERVED,)), dma((SERVED,)), dma((SERVED,)),
            dma((SHARES - 1,)), dma((SHARES - 1,)), dma((SERVED * SHARES,)), dma((GROUPS,)),
        ],
        compiler_params=pltpu.CompilerParams(collective_id=0, has_side_effects=True),
        name="beam_scores",
    )(queries, node_table, beam, w_query, w_node, w_cross, vectors)


def solution(mesh):
    in_specs = (
        P("blk", None),
        P("blk", None),
        P("blk", None),
        P(None, "hid"),
        P(None, "hid"),
        P(None, "hid"),
        P("hid"),
        P("hid"),
    )
    return jax.shard_map(shards, mesh=mesh, in_specs=in_specs, out_specs=P("blk", "hid"), check_vma=False)
```

time: 197 us -> 49.2 us (0.25)
  the two profiles are of different devices: /device:TPU:1 before, /device:TPU:17 now
where the time goes in v1:
time: 49.2 us; the launch traced here: 48.9 us
  Pallas kernels  43.3 us (88%)
  local copies, waits for them, and re-layouts  5.03 us (10%)
  other arithmetic  0.57 us (1%)
    pallas_call x1, Pallas kernels, shards(): pl.pallas_call(kernel, out_shape=jax.ShapeDtypeStruct((Q, COLS), F32), in...  43.3 us
    unnamed x11, local copies, waits for them, and re-layouts  3.56 us
    pallas_call x1, local copies, waits for them, and re-layouts, shards(): pl.pallas_call(kernel, out_shape=jax.ShapeDtypeStruct((Q, COLS), F32), in...  1.48 us

profile of v1, /device:TPU:17, one launch (start us, length us, event | category | flops | bytes accessed | tf_op | source)
XLA Modules:
  0.0 48.9 jit_solution(993864347465432629)
XLA Ops:
  0.0 0.0 copy-start.2
  0.0 0.0 copy-start.3
  0.0 0.7 %copy-done.2 = bf16[64]{0:T(256)(128)(2,1)S(1)} copy-done((bf16[64]{0:T(256)(128)(2,1)S(1)}, bf16[64]{0:T(256)(128)(2,1)}, u32[]{:S(2)}) %copy-start.2) | copy-done | bytes 152
  0.7 0.0 copy-done.3
  0.7 0.6 %maximum_convert_fusion.vec_ref = f32[2,64]{1,0:T(2,128)} fusion(bf16[1,64]{1,0:T(2,128)(2,1)S(1)} %bitcast.2, bf16[1,64]{1,0:T(2,128)(2,1)S(1)} %bitcast.3), kind=kLoop, calls=%fused_computation | loop fusion | flops 512 | bytes 768 | tf_op jit(solution)/shard_map/convert_element_type | solution.py:300
  1.2 0.0 copy-start
  1.2 1.4 %copy.9.wq_ref = bf16[128,64]{1,0:T(8,128)(2,1)} copy(bf16[128,64]{0,1:T(8,128)(2,1)} %param.11) | data formatting | bytes 32768 | tf_op args[3]
  2.7 0.0 copy-done
  2.7 0.0 copy-start.1
  2.7 0.7 %copy.10.wn_ref = bf16[128,64]{1,0:T(8,128)(2,1)} copy(bf16[128,64]{0,1:T(8,128)(2,1)S(1)} %copy-done) | data formatting | bytes 32768 | tf_op args[4]
  3.4 0.0 copy-done.1
  3.4 0.7 %copy.11.wc_ref = bf16[128,64]{1,0:T(8,128)(2,1)} copy(bf16[128,64]{0,1:T(8,128)(2,1)S(1)} %copy-done.1) | data formatting | bytes 32768 | tf_op args[5]
  4.1 43.3 %beam_scores.1 = f32[96,32]{1,0:T(8,128)} custom-call(bf16[96,128]{1,0:T(8,128)(2,1)} %q_ref.1, bf16[2048,128]{1,0:T(8,128)(2,1)} %table_ref.1, s32[96,128]{1,0:T(8,128)} %beam_ref.1, bf16[128,64]{1,0:T(8,128)(2,1)} %copy.9.wq_ref, bf16[128,64]{1,0:T(8,128)(2,1)} %copy.10.wn_ref, bf16[128,64]{1,0:T(8,128)(2,1)} %copy.11.wc_ref, ...), custom_call_target="tpu_custom_call" | custom-call | tf_op jit(solution)/shard_map/beam_scores/pallas_call | solution.py:302
  47.4 1.5 %copy.12 = f32[96,32]{0,1:T(8,128)} copy(f32[96,32]{1,0:T(8,128)} %beam_scores.1) | data formatting | bytes 24576 | tf_op jit(solution)/shard_map/beam_scores/pallas_call | solution.py:302
Async XLA Ops:
  0.0 0.7 %copy-start.2 = (bf16[64]{0:T(256)(128)(2,1)S(1)}, bf16[64]{0:T(256)(128)(2,1)}, u32[]{:S(2)}) copy-start(bf16[64]{0:T(256)(128)(2,1)} %param.15) | copy-start | bytes 388
  0.0 0.7 %copy-start.3 = (bf16[64]{0:T(256)(128)(2,1)S(1)}, bf16[64]{0:T(256)(128)(2,1)}, u32[]{:S(2)}) copy-start(bf16[64]{0:T(256)(128)(2,1)} %param.14) | copy-start | bytes 388
  1.2 1.4 %copy-start = (bf16[128,64]{0,1:T(8,128)(2,1)S(1)}, bf16[128,64]{0,1:T(8,128)(2,1)}, u32[]{:S(2)}) copy-start(bf16[128,64]{0,1:T(8,128)(2,1)} %param.12) | copy-start | bytes 49156
  2.7 0.7 %copy-start.1 = (bf16[128,64]{0,1:T(8,128)(2,1)S(1)}, bf16[128,64]{0,1:T(8,128)(2,1)}, u32[]{:S(2)}) copy-start(bf16[128,64]{0,1:T(8,128)(2,1)} %param.13) | copy-start | bytes 49156

commit v2 on v1

v2 whole, which is shorter than its diff:
```python
import functools

import jax
import jax.numpy as jnp
from jax import lax
from jax.experimental import pallas as pl
from jax.experimental.pallas import tpu as pltpu
from jax.sharding import PartitionSpec as P

BF16, F32, I32 = jnp.bfloat16, jnp.float32, jnp.int32
GROUPS = 32
SHARES = 4
SERVED = GROUPS // SHARES
Q = 96
BEAM = 128
D = 128
HID = 256
HID_DEV = HID // SHARES
PARENTS = 1024
ROWS = 3
SLOTS = ROWS * 128
COLS = BEAM // SHARES
PAIR = 2
MESH = pl.DeviceIdType.MESH


def nt(a, b):
    return lax.dot_general(a, b, (((1,), (1,)), ((), ())), preferred_element_type=F32)


def nn(a, b):
    return jnp.dot(a, b, preferred_element_type=F32)


def iota(shape, dim):
    return lax.broadcasted_iota(I32, shape, dim)


def flag(cond):
    return jnp.where(cond, 1.0, 0.0).astype(BF16)


def eye(n):
    return flag(iota((n, n), 0) == iota((n, n), 1))


def wide_row(row, copies):
    return jnp.concatenate([jnp.broadcast_to(row, (16, row.shape[1])).astype(BF16)] * copies, axis=0)


def one_hot(row, height):
    row = wide_row(row, height // 16)
    return jnp.where(iota((height, row.shape[1]), 0).astype(F32).astype(BF16) == row, 1.0, 0.0).astype(BF16)


def list_starts(owner, even, ids):
    lower = flag(iota((Q, Q), 0) > iota((Q, Q), 1))
    ones = jnp.ones((BEAM, BEAM), BF16)
    masks = [flag((owner == o) & even) for o in ids]
    before = nn(lower, jnp.concatenate(masks, axis=1))
    tall = [
        before[:, i * BEAM : (i + 1) * BEAM] - jnp.where((owner < o) & even, 1.0, 0.0) for i, o in enumerate(ids)
    ]
    total = nn(jnp.concatenate(tall, axis=0).astype(BF16), ones)
    picked = jnp.zeros((Q, BEAM), F32)
    for i, o in enumerate(ids):
        picked = jnp.where(owner == o, total[i * Q : (i + 1) * Q], picked)
    return picked.astype(I32)


def kernel(
    q_hbm, table_hbm, beam_hbm, wq_hbm, wn_hbm, wc_hbm, bias_hbm, wout_hbm, out_ref,
    q_ref, table_ref, beam_ref, w_in, bias_in, wout_in,
    w_all, qbuf, req, reqbuf, ret, retbuf, tt, t32, inner, code_s, jl_s, a_s, b_s, wo_s, bi_s,
    in_sem, q_send, q_recv, r_send, r_recv, w_send, w_recv, s_send, s_recv,
):
    b, h = lax.axis_index("blk"), lax.axis_index("hid")
    y, xh, z = b // 8, (b // 4) % 2, b % 4
    xl, core = h // 2, h % 2
    my_server = (y % 2) * 2 + z % 2
    my_place = (y // 2) * 4 + xh * 2 + z // 2
    own_xh = (xh + xl + y) % 2
    own_zl = 1 - core

    def owner_of(i):
        return (i // 2) * 8 + own_xh * 4 + (i % 2) * 2 + own_zl

    def source_of(k):
        return ((k // 4) * 2 + xl) * 8 + ((k // 2) % 2) * 4 + (k % 2) * 2 + core

    loads = [
        pltpu.make_async_copy(src, dst, in_sem.at[n])
        for n, (src, dst) in enumerate((
            (beam_hbm, beam_ref), (wn_hbm, w_in.at[0]), (wc_hbm, w_in.at[1]), (wq_hbm, w_in.at[2]),
            (bias_hbm, bias_in), (wout_hbm, wout_in), (q_hbm, q_ref), (table_hbm, table_ref),
        ))
    ]
    for load in loads:
        load.start()

    barrier = pltpu.get_barrier_semaphore()
    served_self = my_server == h

    @pl.loop(0, GROUPS)
    def _(o):
        @pl.when(jnp.logical_not(served_self & (o == b)))
        def _():
            pl.semaphore_signal(barrier, inc=1, device_id={"blk": o, "hid": my_server}, device_id_type=MESH)

    @pl.loop(0, SERVED)
    def _(k):
        sender = lax.rem(xl + xh + (k // 2) % 2, 2) * 2 + 1 - z % 2
        pl.semaphore_signal(barrier, inc=1, device_id={"blk": source_of(k), "hid": sender}, device_id_type=MESH)

    for d in range(1, SHARES):
        pl.semaphore_signal(barrier, inc=1, device_id={"blk": b, "hid": (h + d) % SHARES}, device_id_type=MESH)

    for load in loads[:7]:
        load.wait()

    beam = beam_ref[...]
    even = (beam & 1) == 0
    parent = beam >> 1
    owner = beam >> 11
    local = parent & (PARENTS - 1)
    keys = jnp.where(even, parent, 1 << 20)

    def count(step, acc):
        for u in range(8):
            acc = acc + jnp.where(pltpu.roll(keys, 8 * step + u, 1) < parent, 1, 0)
        return acc

    below = lax.fori_loop(0, BEAM // 8, count, jnp.zeros((Q, BEAM), I32), unroll=False)
    inner[...] = below

    asked = ((owner >> 2) & 1 == own_xh) & ((owner & 1) == own_zl)
    group = jnp.where(asked, (owner >> 3) * 2 + ((owner >> 1) & 1), 64)
    rank = below + list_starts(owner, even, [owner_of(i) for i in range(SERVED)])
    code_s[...] = jnp.where(even & asked, group * 4 + (rank >> 7), 64).astype(F32)
    jl_s[...] = (rank & 127).astype(F32)
    a_s[...] = (local & 255).astype(F32)
    b_s[...] = (iota((Q, BEAM), 0) + 96 * (local >> 8) - 192).astype(F32)

    row64 = iota((64, BEAM), 0)
    target = ((row64 >> 3) * 4 + (row64 & 3)).astype(F32).astype(BF16)
    is_b = ((iota((16, BEAM), 0) >> 2) & 1).astype(F32).astype(BF16)
    is_a = 1 - is_b

    def compact(step, acc):
        values, places = [], []
        for u in range(16):
            at = pl.ds(16 * step + u, 1)
            payload = is_a * wide_row(a_s[at, :], 1) + is_b * wide_row(b_s[at, :], 1)
            payload = jnp.concatenate([payload] * 4, axis=0)
            values.append(jnp.where(wide_row(code_s[at, :], 4) == target, payload, 0.0).astype(BF16))
            places.append(one_hot(jl_s[at, :], BEAM))
        return acc + nt(jnp.concatenate(values, axis=1), jnp.concatenate(places, axis=1))

    tables = lax.fori_loop(0, Q // 16, compact, jnp.zeros((64, BEAM), F32), unroll=False)
    for i in range(SERVED):
        req[i] = tables[8 * i : 8 * i + 8]

    ident = eye(HID_DEV)
    vectors = jnp.concatenate(
        [jnp.broadcast_to(v[...].astype(F32), (64, HID_DEV)) for v in (bias_in, wout_in)], axis=0
    ).astype(BF16)
    my_rows = pl.ds(pl.multiple_of(h * HID_DEV, HID_DEV), HID_DEV)
    for n in range(3):
        w_all[my_rows, n * D : (n + 1) * D] = w_in[n]
    w_all[my_rows, 3 * D :] = nt(ident, vectors).astype(BF16)

    pl.semaphore_wait(barrier, GROUPS + SERVED + SHARES - 1 - jnp.where(served_self, 1, 0))

    def q_copy(i):
        return pltpu.make_async_remote_copy(
            src_ref=q_ref, dst_ref=qbuf.at[my_place], send_sem=q_send.at[i], recv_sem=q_recv.at[my_place],
            device_id={"blk": owner_of(i), "hid": my_server}, device_id_type=MESH,
        )

    def r_copy(i):
        return pltpu.make_async_remote_copy(
            src_ref=req.at[i], dst_ref=reqbuf.at[my_place], send_sem=r_send.at[i], recv_sem=r_recv.at[my_place],
            device_id={"blk": owner_of(i), "hid": my_server}, device_id_type=MESH,
        )

    def w_copy(d):
        return pltpu.make_async_remote_copy(
            src_ref=w_all.at[my_rows], dst_ref=w_all.at[my_rows], send_sem=w_send.at[d - 1], recv_sem=w_recv.at[d - 1],
            device_id={"blk": b, "hid": (h + d) % SHARES}, device_id_type=MESH,
        )

    @pl.loop(0, SERVED)
    def _(i):
        q_copy(i).start()
        r_copy(i).start()

    for d in range(1, SHARES):
        w_copy(d).start()

    loads[7].wait()
    t32[...] = table_ref[...].astype(F32)
    ident = eye(D)
    for child in range(2):
        half = t32[pl.ds(child, PARENTS, stride=2), :].astype(BF16)
        tt[child * D : (child + 1) * D, :] = nt(ident, half).astype(BF16)

    def all_owners(g, acc):
        return acc + list_starts(owner, even, [g * SERVED + i for i in range(SERVED)])

    rank = lax.fori_loop(0, GROUPS // SERVED, all_owners, inner[...], unroll=False)
    code = owner * 8 + (beam & 1) * 4 + (rank >> 7)
    mine = flag(iota((COLS, BEAM), 1) == iota((COLS, BEAM), 0) + h * COLS)
    pad = jnp.zeros((BEAM - Q, BEAM), F32)

    def columns(values):
        return nt(mine, jnp.concatenate([values.astype(F32), pad], axis=0).astype(BF16))

    code_t, jl_t = columns(code), columns(rank & 127)

    for d in range(1, SHARES):
        w_copy(d).wait_recv()
    bi_s[...] = jnp.broadcast_to(w_all[:, 3 * D : 3 * D + 1].astype(F32), (HID, 128))
    wo_s[...] = jnp.broadcast_to(w_all[:, 3 * D + 64 : 3 * D + 65].astype(F32), (HID, 128))

    def s_copy(k, d):
        return pltpu.make_async_remote_copy(
            src_ref=ret.at[k], dst_ref=retbuf.at[b], send_sem=s_send.at[k * SHARES + d], recv_sem=s_recv.at[b],
            device_id={"blk": source_of(k), "hid": d}, device_id_type=MESH,
        )

    def score(k):
        digits = reqbuf[k]
        low, rest = digits[0:4], digits[4:8] + 192.0
        high = jnp.where(rest >= 96.0, 1.0, 0.0) + jnp.where(rest >= 192.0, 1.0, 0.0) + jnp.where(rest >= 288.0, 1.0, 0.0)
        asking = rest - 96.0 * high
        wanted = low + 256.0 * high
        asking = jnp.concatenate([asking[r : r + 1] for r in range(ROWS)], axis=1)
        wanted = jnp.concatenate([wanted[r : r + 1] for r in range(ROWS)], axis=1)
        hot = jnp.concatenate([one_hot(wanted - 256.0 * c, 256) for c in range(PARENTS // 256)], axis=0)
        found = nn(tt[...], hot)
        query = nn(nt(eye(D), qbuf[k]).astype(BF16), one_hot(asking, Q))
        bias = jnp.concatenate([bi_s[...]] * ROWS, axis=1)
        weight = jnp.concatenate([wo_s[...]] * ROWS, axis=1)
        shared = nn(w_all[:, 2 * D : 3 * D], query.astype(BF16)) + bias
        rows = []
        for child in range(2):
            node = found[child * D : (child + 1) * D]
            joined = jnp.concatenate([node.astype(BF16), (node * query).astype(BF16)], axis=0)
            hidden = jnp.maximum(nn(w_all[:, : 2 * D], joined) + shared, 0.0)
            total = jnp.sum(hidden * weight, axis=0, keepdims=True)
            rows += [total[:, r * 128 : (r + 1) * 128] for r in range(ROWS)] + [jnp.zeros((1, 128), F32)]
        return jnp.concatenate(rows, axis=0)

    @pl.loop(0, SERVED // PAIR)
    def _(pair):
        for u in range(PAIR):
            k = PAIR * pair + u
            pltpu.make_async_remote_copy(
                src_ref=q_ref, dst_ref=qbuf.at[k], send_sem=q_send.at[k], recv_sem=q_recv.at[k],
                device_id={"blk": source_of(k), "hid": (h + 1) % SHARES}, device_id_type=MESH,
            ).wait_recv()
            pltpu.make_async_remote_copy(
                src_ref=req.at[k], dst_ref=reqbuf.at[k], send_sem=r_send.at[k], recv_sem=r_recv.at[k],
                device_id={"blk": source_of(k), "hid": (h + 1) % SHARES}, device_id_type=MESH,
            ).wait_recv()
        for u in range(PAIR):
            ret[PAIR * pair + u] = score(PAIR * pair + u)
        for u in range(PAIR):
            k = PAIR * pair + u
            for d in range(SHARES):
                here = (d == h) & (source_of(k) == b)

                @pl.when(here)
                def _():
                    retbuf[b] = ret[k]

                @pl.when(jnp.logical_not(here))
                def _():
                    s_copy(k, d).start()

    @pl.loop(0, GROUPS)
    def _(o):
        @pl.when(jnp.logical_not(served_self & (o == b)))
        def _():
            pltpu.make_async_remote_copy(
                src_ref=ret.at[0], dst_ref=retbuf.at[o], send_sem=s_send.at[0], recv_sem=s_recv.at[o],
                device_id={"blk": b, "hid": (h + 1) % SHARES}, device_id_type=MESH,
            ).wait_recv()

    table = retbuf[...].reshape(GROUPS * 8, 128)
    coarse = table.astype(BF16)
    fine = (table - coarse.astype(F32)).astype(BF16)
    slot_row = iota((GROUPS * 8, 2 * 128), 0).astype(F32)
    for c in range(0, COLS, 2):
        hot = one_hot(jnp.concatenate([jl_t[c : c + 1], jl_t[c + 1 : c + 2]], axis=1), 128)
        which = jnp.concatenate([code_t[c : c + 1], code_t[c + 1 : c + 2]], axis=1)
        seen = nn(coarse, hot) + nn(fine, hot)
        total = jnp.sum(jnp.where(slot_row == which, seen, 0.0), axis=0, keepdims=True)
        out_ref[c : c + 1, :] = total[:, :Q]
        out_ref[c + 1 : c + 2, :] = total[:, 128 : 128 + Q]

    @pl.loop(0, SERVED)
    def _(i):
        q_copy(i).wait_send()
        r_copy(i).wait_send()
        for d in range(SHARES):
            @pl.when(jnp.logical_not((d == h) & (source_of(i) == b)))
            def _():
                s_copy(i, d).wait_send()

    for d in range(1, SHARES):
        w_copy(d).wait_send()


def shards(queries, node_table, beam, w_query, w_node, w_cross, bias_hidden, w_out):
    dma = pltpu.SemaphoreType.DMA
    scores = pl.pallas_call(
        kernel,
        out_shape=jax.ShapeDtypeStruct((COLS, Q), F32),
        in_specs=[pl.BlockSpec(memory_space=pl.ANY)] * 8,
        out_specs=pl.BlockSpec(memory_space=pltpu.VMEM),
        scratch_shapes=[
            pltpu.VMEM((Q, D), BF16),
            pltpu.VMEM((2 * PARENTS, D), BF16),
            pltpu.VMEM((Q, BEAM), I32),
            pltpu.VMEM((3, HID_DEV, D), BF16),
            pltpu.VMEM((1, HID_DEV), BF16),
            pltpu.VMEM((1, HID_DEV), BF16),
            pltpu.VMEM((HID, 4 * D), BF16),
            pltpu.VMEM((SERVED, Q, D), BF16),
            pltpu.VMEM((SERVED, 8, 128), F32),
            pltpu.VMEM((SERVED, 8, 128), F32),
            pltpu.VMEM((SERVED, 8, 128), F32),
            pltpu.VMEM((GROUPS, 8, 128), F32),
            pltpu.VMEM((2 * D, PARENTS), BF16),
            pltpu.VMEM((2 * PARENTS, D), F32),
            pltpu.VMEM((Q, BEAM), I32),
            pltpu.VMEM((Q, BEAM), F32),
            pltpu.VMEM((Q, BEAM), F32),
            pltpu.VMEM((Q, BEAM), F32),
            pltpu.VMEM((Q, BEAM), F32),
            pltpu.VMEM((HID, 128), F32),
            pltpu.VMEM((HID, 128), F32),
            dma((8,)), dma((SERVED,)), dma((SERVED,)), dma((SERVED,)), dma((SERVED,)),
            dma((SHARES - 1,)), dma((SHARES - 1,)), dma((SERVED * SHARES,)), dma((GROUPS,)),
        ],
        compiler_params=pltpu.CompilerParams(collective_id=0, has_side_effects=True),
        name="beam_scores",
    )(
        queries, node_table, beam, w_query.T, w_node.T, w_cross.T,
        bias_hidden.reshape(1, HID_DEV), w_out.reshape(1, HID_DEV),
    )
    return scores.T


def solution(mesh):
    in_specs = (
        P("blk", None),
        P("blk", None),
        P("blk", None),
        P(None, "hid"),
        P(None, "hid"),
        P(None, "hid"),
        P("hid"),
        P("hid"),
    )
    return jax.shard_map(shards, mesh=mesh, in_specs=in_specs, out_specs=P("blk", "hid"), check_vma=False)
```

time: 49.2 us -> 32.9 us (0.67)
  the two profiles are of different devices: /device:TPU:17 before, /device:TPU:29 now
where the time goes in v2:
time: 32.9 us; the launch traced here: 32.7 us
  Pallas kernels  31.4 us (95%)
  local copies, waits for them, and re-layouts  1.32 us (4%)
    pallas_call x1, Pallas kernels, shards(): pl.pallas_call(kernel, out_shape=jax.ShapeDtypeStruct((COLS, Q), F32), in...  31.4 us
    unnamed x1, local copies, waits for them, and re-layouts  1.32 us

profile of v2, /device:TPU:29, one launch (start us, length us, event | category | flops | bytes accessed | tf_op | source)
XLA Modules:
  0.0 32.7 jit_solution(8240618850429301477)
XLA Ops:
  0.0 31.4 %beam_scores.1 = f32[32,96]{1,0:T(8,128)} custom-call(bf16[96,128]{1,0:T(8,128)(2,1)} %q_hbm.1, bf16[2048,128]{1,0:T(8,128)(2,1)} %table_hbm.1, s32[96,128]{1,0:T(8,128)} %beam_hbm.1, bf16[64,128]{1,0:T(8,128)(2,1)} %bitcast.7, bf16[64,128]{1,0:T(8,128)(2,1)} %bitcast.8, bf16[64,128]{1,0:T(8,128)(2,1)} %bitcast.9, bf16[1,64]{1,0:T(2,128)(2,1)} %bitcast.10, ...), custom_call_target="tpu_custom_call" | custom-call | tf_op jit(solution)/shard_map/beam_scores/pallas_call | solution.py:317
  31.4 1.3 %copy.10 = f32[96,32]{0,1:T(8,128)} copy(f32[96,32]{0,1:T(8,128)} %bitcast.6) | data formatting | bytes 24576

commit v3 on v2

--- a/solution.py
+++ b/solution.py
@@ -8,6 +8,7 @@
 from jax.sharding import PartitionSpec as P
 
 BF16, F32, I32 = jnp.bfloat16, jnp.float32, jnp.int32
+RANK = jnp.int16
 GROUPS = 32
 SHARES = 4
 SERVED = GROUPS // SHARES
@@ -20,6 +21,7 @@
 ROWS = 3
 SLOTS = ROWS * 128
 COLS = BEAM // SHARES
+STEP = 32
 PAIR = 2
 MESH = pl.DeviceIdType.MESH
 
@@ -50,7 +52,8 @@
 
 def one_hot(row, height):
     row = wide_row(row, height // 16)
-    return jnp.where(iota((height, row.shape[1]), 0).astype(F32).astype(BF16) == row, 1.0, 0.0).astype(BF16)
+    match = iota((height, row.shape[1]), 0).astype(F32).astype(BF16) == row
+    return jnp.where(match, jnp.ones(row.shape, BF16), jnp.zeros(row.shape, BF16))
 
 
 def list_starts(owner, even, ids):
@@ -71,7 +74,7 @@
 def kernel(
     q_hbm, table_hbm, beam_hbm, wq_hbm, wn_hbm, wc_hbm, bias_hbm, wout_hbm, out_ref,
     q_ref, table_ref, beam_ref, w_in, bias_in, wout_in,
-    w_all, qbuf, req, reqbuf, ret, retbuf, tt, t32, inner, code_s, jl_s, a_s, b_s, wo_s, bi_s,
+    w_all, qbuf, req, reqbuf, ret, retbuf, tt, t32, keys, inner, code_s, jl_s, a_s, b_s, wo_s, bi_s,
     in_sem, q_send, q_recv, r_send, r_recv, w_send, w_recv, s_send, s_recv,
 ):
     b, h = lax.axis_index("blk"), lax.axis_index("hid")
@@ -101,14 +104,7 @@
     barrier = pltpu.get_barrier_semaphore()
     served_self = my_server == h
 
-    @pl.loop(0, GROUPS)
-    def _(o):
-        @pl.when(jnp.logical_not(served_self & (o == b)))
-        def _():
-            pl.semaphore_signal(barrier, inc=1, device_id={"blk": o, "hid": my_server}, device_id_type=MESH)
-
-    @pl.loop(0, SERVED)
-    def _(k):
+    for k in range(SERVED):
         sender = lax.rem(xl + xh + (k // 2) % 2, 2) * 2 + 1 - z % 2
         pl.semaphore_signal(barrier, inc=1, device_id={"blk": source_of(k), "hid": sender}, device_id_type=MESH)
 
@@ -120,17 +116,21 @@
 
     beam = beam_ref[...]
     even = (beam & 1) == 0
-    parent = beam >> 1
     owner = beam >> 11
-    local = parent & (PARENTS - 1)
-    keys = jnp.where(even, parent, 1 << 20)
+    local = (beam >> 1) & (PARENTS - 1)
+    tall = jnp.concatenate([beam, jnp.zeros((BEAM - Q, BEAM), I32)], axis=0).T
+    parent = (tall >> 1).astype(RANK)
+    keys[...] = jnp.where((tall & 1) == 0, tall >> 1, 32767)
 
     def count(step, acc):
-        for u in range(8):
-            acc = acc + jnp.where(pltpu.roll(keys, 8 * step + u, 1) < parent, 1, 0)
+        for u in range(16):
+            row = jnp.broadcast_to(keys[pl.ds(16 * step + u, 1), :], (16, 128)).astype(RANK)
+            row = jnp.concatenate([row] * 8, axis=0)
+            acc = acc + jnp.where(row < parent, jnp.ones(acc.shape, RANK), jnp.zeros(acc.shape, RANK))
         return acc
 
-    below = lax.fori_loop(0, BEAM // 8, count, jnp.zeros((Q, BEAM), I32), unroll=False)
+    below = lax.fori_loop(0, BEAM // 16, count, jnp.zeros((BEAM, BEAM), RANK), unroll=False)
+    below = below.astype(I32).T[:Q]
     inner[...] = below
 
     asked = ((owner >> 2) & 1 == own_xh) & ((owner & 1) == own_zl)
@@ -148,15 +148,15 @@
 
     def compact(step, acc):
         values, places = [], []
-        for u in range(16):
-            at = pl.ds(16 * step + u, 1)
+        for u in range(STEP):
+            at = pl.ds(STEP * step + u, 1)
             payload = is_a * wide_row(a_s[at, :], 1) + is_b * wide_row(b_s[at, :], 1)
             payload = jnp.concatenate([payload] * 4, axis=0)
             values.append(jnp.where(wide_row(code_s[at, :], 4) == target, payload, 0.0).astype(BF16))
             places.append(one_hot(jl_s[at, :], BEAM))
         return acc + nt(jnp.concatenate(values, axis=1), jnp.concatenate(places, axis=1))
 
-    tables = lax.fori_loop(0, Q // 16, compact, jnp.zeros((64, BEAM), F32), unroll=False)
+    tables = lax.fori_loop(0, Q // STEP, compact, jnp.zeros((64, BEAM), F32), unroll=False)
     for i in range(SERVED):
         req[i] = tables[8 * i : 8 * i + 8]
 
@@ -169,7 +169,7 @@
         w_all[my_rows, n * D : (n + 1) * D] = w_in[n]
     w_all[my_rows, 3 * D :] = nt(ident, vectors).astype(BF16)
 
-    pl.semaphore_wait(barrier, GROUPS + SERVED + SHARES - 1 - jnp.where(served_self, 1, 0))
+    pl.semaphore_wait(barrier, SERVED + SHARES - 1)
 
     def q_copy(i):
         return pltpu.make_async_remote_copy(
@@ -189,13 +189,14 @@
             device_id={"blk": b, "hid": (h + d) % SHARES}, device_id_type=MESH,
         )
 
+    for d in range(1, SHARES):
+        w_copy(d).start()
+
     @pl.loop(0, SERVED)
-    def _(i):
+    def _(n):
+        i = lax.rem(y + 2 + n // 2, 4) * 2 + lax.rem(z // 2 + 1 + n, 2)
         q_copy(i).start()
         r_copy(i).start()
-
-    for d in range(1, SHARES):
-        w_copy(d).start()
 
     loads[7].wait()
     t32[...] = table_ref[...].astype(F32)
@@ -208,19 +209,14 @@
         return acc + list_starts(owner, even, [g * SERVED + i for i in range(SERVED)])
 
     rank = lax.fori_loop(0, GROUPS // SERVED, all_owners, inner[...], unroll=False)
-    code = owner * 8 + (beam & 1) * 4 + (rank >> 7)
+    code = owner * 4 + (rank >> 7)
     mine = flag(iota((COLS, BEAM), 1) == iota((COLS, BEAM), 0) + h * COLS)
     pad = jnp.zeros((BEAM - Q, BEAM), F32)
 
     def columns(values):
         return nt(mine, jnp.concatenate([values.astype(F32), pad], axis=0).astype(BF16))
 
-    code_t, jl_t = columns(code), columns(rank & 127)
-
-    for d in range(1, SHARES):
-        w_copy(d).wait_recv()
-    bi_s[...] = jnp.broadcast_to(w_all[:, 3 * D : 3 * D + 1].astype(F32), (HID, 128))
-    wo_s[...] = jnp.broadcast_to(w_all[:, 3 * D + 64 : 3 * D + 65].astype(F32), (HID, 128))
+    code_t, jl_t = columns(code), columns((beam & 1) * 128 + (rank & 127))
 
     def s_copy(k, d):
         return pltpu.make_async_remote_copy(
@@ -228,7 +224,7 @@
             device_id={"blk": source_of(k), "hid": d}, device_id_type=MESH,
         )
 
-    def score(k):
+    def gather(k):
         digits = reqbuf[k]
         low, rest = digits[0:4], digits[4:8] + 192.0
         high = jnp.where(rest >= 96.0, 1.0, 0.0) + jnp.where(rest >= 192.0, 1.0, 0.0) + jnp.where(rest >= 288.0, 1.0, 0.0)
@@ -239,6 +235,9 @@
         hot = jnp.concatenate([one_hot(wanted - 256.0 * c, 256) for c in range(PARENTS // 256)], axis=0)
         found = nn(tt[...], hot)
         query = nn(nt(eye(D), qbuf[k]).astype(BF16), one_hot(asking, Q))
+        return found, query
+
+    def score(found, query):
         bias = jnp.concatenate([bi_s[...]] * ROWS, axis=1)
         weight = jnp.concatenate([wo_s[...]] * ROWS, axis=1)
         shared = nn(w_all[:, 2 * D : 3 * D], query.astype(BF16)) + bias
@@ -251,10 +250,15 @@
             rows += [total[:, r * 128 : (r + 1) * 128] for r in range(ROWS)] + [jnp.zeros((1, 128), F32)]
         return jnp.concatenate(rows, axis=0)
 
+    def near(n):
+        a = lax.rem(y // 2 + n // 4, 2)
+        e = lax.rem(xh + n, 2)
+        return a * 4 + e * 2 + lax.rem(z // 2 + n // 2, 2)
+
     @pl.loop(0, SERVED // PAIR)
     def _(pair):
-        for u in range(PAIR):
-            k = PAIR * pair + u
+        places = [near(PAIR * pair + u) for u in range(PAIR)]
+        for k in places:
             pltpu.make_async_remote_copy(
                 src_ref=q_ref, dst_ref=qbuf.at[k], send_sem=q_send.at[k], recv_sem=q_recv.at[k],
                 device_id={"blk": source_of(k), "hid": (h + 1) % SHARES}, device_id_type=MESH,
@@ -263,10 +267,18 @@
                 src_ref=req.at[k], dst_ref=reqbuf.at[k], send_sem=r_send.at[k], recv_sem=r_recv.at[k],
                 device_id={"blk": source_of(k), "hid": (h + 1) % SHARES}, device_id_type=MESH,
             ).wait_recv()
-        for u in range(PAIR):
-            ret[PAIR * pair + u] = score(PAIR * pair + u)
-        for u in range(PAIR):
-            k = PAIR * pair + u
+        gathered = [gather(k) for k in places]
+
+        @pl.when(pair == 0)
+        def _():
+            for d in range(1, SHARES):
+                w_copy(d).wait_recv()
+            bi_s[...] = jnp.broadcast_to(w_all[:, 3 * D : 3 * D + 1].astype(F32), (HID, 128))
+            wo_s[...] = jnp.broadcast_to(w_all[:, 3 * D + 64 : 3 * D + 65].astype(F32), (HID, 128))
+
+        for k, (found, query) in zip(places, gathered):
+            ret[k] = score(found, query)
+        for k in places:
             for d in range(SHARES):
                 here = (d == h) & (source_of(k) == b)
 
@@ -287,14 +299,17 @@
                 device_id={"blk": b, "hid": (h + 1) % SHARES}, device_id_type=MESH,
             ).wait_recv()
 
-    table = retbuf[...].reshape(GROUPS * 8, 128)
+    table = jnp.concatenate(
+        [retbuf[:, 4 * child : 4 * child + 4, :].reshape(GROUPS * 4, 128) for child in range(2)], axis=1
+    )
     coarse = table.astype(BF16)
-    fine = (table - coarse.astype(F32)).astype(BF16)
-    slot_row = iota((GROUPS * 8, 2 * 128), 0).astype(F32)
+    parts = jnp.concatenate([coarse, (table - coarse.astype(F32)).astype(BF16)], axis=0)
+    slot_row = iota((GROUPS * 4, 2 * 128), 0).astype(F32)
     for c in range(0, COLS, 2):
-        hot = one_hot(jnp.concatenate([jl_t[c : c + 1], jl_t[c + 1 : c + 2]], axis=1), 128)
+        hot = one_hot(jnp.concatenate([jl_t[c : c + 1], jl_t[c + 1 : c + 2]], axis=1), 256)
         which = jnp.concatenate([code_t[c : c + 1], code_t[c + 1 : c + 2]], axis=1)
-        seen = nn(coarse, hot) + nn(fine, hot)
+        seen = nn(parts, hot)
+        seen = seen[: GROUPS * 4] + seen[GROUPS * 4 :]
         total = jnp.sum(jnp.where(slot_row == which, seen, 0.0), axis=0, keepdims=True)
         out_ref[c : c + 1, :] = total[:, :Q]
         out_ref[c + 1 : c + 2, :] = total[:, 128 : 128 + Q]
@@ -334,6 +349,7 @@
             pltpu.VMEM((GROUPS, 8, 128), F32),
             pltpu.VMEM((2 * D, PARENTS), BF16),
             pltpu.VMEM((2 * PARENTS, D), F32),
+            pltpu.VMEM((BEAM, BEAM), I32),
             pltpu.VMEM((Q, BEAM), I32),
             pltpu.VMEM((Q, BEAM), F32),
             pltpu.VMEM((Q, BEAM), F32),

time: 32.9 us -> 32.3 us (0.982)
  the two profiles are of different devices: /device:TPU:29 before, /device:TPU:1 now
where the time goes in v3:
time: 32.3 us; the launch traced here: 32.1 us
  Pallas kernels  30.8 us (95%)
  local copies, waits for them, and re-layouts  1.32 us (4%)
    pallas_call x1, Pallas kernels, shards(): pl.pallas_call(kernel, out_shape=jax.ShapeDtypeStruct((COLS, Q), F32), in...  30.8 us
    unnamed x1, local copies, waits for them, and re-layouts  1.32 us

profile of v3, /device:TPU:1, one launch (start us, length us, event | category | flops | bytes accessed | tf_op | source)
XLA Modules:
  0.0 32.1 jit_solution(1903112664451031185)
XLA Ops:
  0.0 30.8 %beam_scores.1 = f32[32,96]{1,0:T(8,128)} custom-call(bf16[96,128]{1,0:T(8,128)(2,1)} %q_hbm.1, bf16[2048,128]{1,0:T(8,128)(2,1)} %table_hbm.1, s32[96,128]{1,0:T(8,128)} %beam_hbm.1, bf16[64,128]{1,0:T(8,128)(2,1)} %bitcast.7, bf16[64,128]{1,0:T(8,128)(2,1)} %bitcast.8, bf16[64,128]{1,0:T(8,128)(2,1)} %bitcast.9, bf16[1,64]{1,0:T(2,128)(2,1)} %bitcast.10, ...), custom_call_target="tpu_custom_call" | custom-call | tf_op jit(solution)/shard_map/beam_scores/pallas_call | solution.py:332
  30.8 1.3 %copy.10 = f32[96,32]{0,1:T(8,128)} copy(f32[96,32]{0,1:T(8,128)} %bitcast.6) | data formatting | bytes 24576

commit v4 on v3

--- a/solution.py
+++ b/solution.py
@@ -80,16 +80,18 @@
     b, h = lax.axis_index("blk"), lax.axis_index("hid")
     y, xh, z = b // 8, (b // 4) % 2, b % 4
     xl, core = h // 2, h % 2
-    my_server = (y % 2) * 2 + z % 2
     my_place = (y // 2) * 4 + xh * 2 + z // 2
-    own_xh = (xh + xl + y) % 2
+    flip = lax.rem(xh + xl + y, 2)
     own_zl = 1 - core
 
     def owner_of(i):
-        return (i // 2) * 8 + own_xh * 4 + (i % 2) * 2 + own_zl
+        return (i // 2) * 8 + lax.rem(flip + i // 2, 2) * 4 + lax.rem(i, 2) * 2 + own_zl
+
+    def server_of(i):
+        return lax.rem(y + i // 2, 2) * 2 + lax.rem(z, 2)
 
     def source_of(k):
-        return ((k // 4) * 2 + xl) * 8 + ((k // 2) % 2) * 4 + (k % 2) * 2 + core
+        return ((k // 4) * 2 + lax.rem(xl + y, 2)) * 8 + ((k // 2) % 2) * 4 + (k % 2) * 2 + core
 
     loads = [
         pltpu.make_async_copy(src, dst, in_sem.at[n])
@@ -102,7 +104,7 @@
         load.start()
 
     barrier = pltpu.get_barrier_semaphore()
-    served_self = my_server == h
+    served_self = z % 2 == h
 
     for k in range(SERVED):
         sender = lax.rem(xl + xh + (k // 2) % 2, 2) * 2 + 1 - z % 2
@@ -133,13 +135,52 @@
     below = below.astype(I32).T[:Q]
     inner[...] = below
 
-    asked = ((owner >> 2) & 1 == own_xh) & ((owner & 1) == own_zl)
+    asked = (((owner >> 2) + (owner >> 3)) & 1 == flip) & ((owner & 1) == own_zl)
     group = jnp.where(asked, (owner >> 3) * 2 + ((owner >> 1) & 1), 64)
     rank = below + list_starts(owner, even, [owner_of(i) for i in range(SERVED)])
     code_s[...] = jnp.where(even & asked, group * 4 + (rank >> 7), 64).astype(F32)
     jl_s[...] = (rank & 127).astype(F32)
     a_s[...] = (local & 255).astype(F32)
     b_s[...] = (iota((Q, BEAM), 0) + 96 * (local >> 8) - 192).astype(F32)
+
+    ident = eye(HID_DEV)
+    vectors = jnp.concatenate(
+        [jnp.broadcast_to(v[...].astype(F32), (64, HID_DEV)) for v in (bias_in, wout_in)], axis=0
+    ).astype(BF16)
+    my_rows = pl.ds(pl.multiple_of(h * HID_DEV, HID_DEV), HID_DEV)
+    for n in range(3):
+        w_all[my_rows, n * D : (n + 1) * D] = w_in[n]
+    w_all[my_rows, 3 * D :] = nt(ident, vectors).astype(BF16)
+
+    pl.semaphore_wait(barrier, SERVED + SHARES - 1)
+
+    def q_copy(i):
+        return pltpu.make_async_remote_copy(
+            src_ref=q_ref, dst_ref=qbuf.at[my_place], send_sem=q_send.at[i], recv_sem=q_recv.at[my_place],
+            device_id={"blk": owner_of(i), "hid": server_of(i)}, device_id_type=MESH,
+        )
+
+    def r_copy(i):
+        return pltpu.make_async_remote_copy(
+            src_ref=req.at[i], dst_ref=reqbuf.at[my_place], send_sem=r_send.at[i], recv_sem=r_recv.at[my_place],
+            device_id={"blk": owner_of(i), "hid": server_of(i)}, device_id_type=MESH,
+        )
+
+    def w_copy(d):
+        return pltpu.make_async_remote_copy(
+            src_ref=w_all.at[my_rows], dst_ref=w_all.at[my_rows], send_sem=w_send.at[d - 1], recv_sem=w_recv.at[d - 1],
+            device_id={"blk": b, "hid": (h + d) % SHARES}, device_id_type=MESH,
+        )
+
+    for d in range(1, SHARES):
+        w_copy(d).start()
+
+    def far(n):
+        return lax.rem(y + 2 + n // 2, 4) * 2 + lax.rem(z // 2 + 1 + n, 2)
+
+    @pl.loop(0, SERVED)
+    def _(n):
+        q_copy(far(n)).start()
 
     row64 = iota((64, BEAM), 0)
     target = ((row64 >> 3) * 4 + (row64 & 3)).astype(F32).astype(BF16)
@@ -158,45 +199,11 @@
 
     tables = lax.fori_loop(0, Q // STEP, compact, jnp.zeros((64, BEAM), F32), unroll=False)
     for i in range(SERVED):
-        req[i] = tables[8 * i : 8 * i + 8]
-
-    ident = eye(HID_DEV)
-    vectors = jnp.concatenate(
-        [jnp.broadcast_to(v[...].astype(F32), (64, HID_DEV)) for v in (bias_in, wout_in)], axis=0
-    ).astype(BF16)
-    my_rows = pl.ds(pl.multiple_of(h * HID_DEV, HID_DEV), HID_DEV)
-    for n in range(3):
-        w_all[my_rows, n * D : (n + 1) * D] = w_in[n]
-    w_all[my_rows, 3 * D :] = nt(ident, vectors).astype(BF16)
-
-    pl.semaphore_wait(barrier, SERVED + SHARES - 1)
-
-    def q_copy(i):
-        return pltpu.make_async_remote_copy(
-            src_ref=q_ref, dst_ref=qbuf.at[my_place], send_sem=q_send.at[i], recv_sem=q_recv.at[my_place],
-            device_id={"blk": owner_of(i), "hid": my_server}, device_id_type=MESH,
-        )
-
-    def r_copy(i):
-        return pltpu.make_async_remote_copy(
-            src_ref=req.at[i], dst_ref=reqbuf.at[my_place], send_sem=r_send.at[i], recv_sem=r_recv.at[my_place],
-            device_id={"blk": owner_of(i), "hid": my_server}, device_id_type=MESH,
-        )
-
-    def w_copy(d):
-        return pltpu.make_async_remote_copy(
-            src_ref=w_all.at[my_rows], dst_ref=w_all.at[my_rows], send_sem=w_send.at[d - 1], recv_sem=w_recv.at[d - 1],
-            device_id={"blk": b, "hid": (h + d) % SHARES}, device_id_type=MESH,
-        )
-
-    for d in range(1, SHARES):
-        w_copy(d).start()
+        req[i] = tables[8 * i : 8 * i + 8].astype(BF16)
 
     @pl.loop(0, SERVED)
     def _(n):
-        i = lax.rem(y + 2 + n // 2, 4) * 2 + lax.rem(z // 2 + 1 + n, 2)
-        q_copy(i).start()
-        r_copy(i).start()
+        r_copy(far(n)).start()
 
     loads[7].wait()
     t32[...] = table_ref[...].astype(F32)
@@ -205,50 +212,47 @@
         half = t32[pl.ds(child, PARENTS, stride=2), :].astype(BF16)
         tt[child * D : (child + 1) * D, :] = nt(ident, half).astype(BF16)
 
-    def all_owners(g, acc):
-        return acc + list_starts(owner, even, [g * SERVED + i for i in range(SERVED)])
-
-    rank = lax.fori_loop(0, GROUPS // SERVED, all_owners, inner[...], unroll=False)
-    code = owner * 4 + (rank >> 7)
-    mine = flag(iota((COLS, BEAM), 1) == iota((COLS, BEAM), 0) + h * COLS)
-    pad = jnp.zeros((BEAM - Q, BEAM), F32)
-
-    def columns(values):
-        return nt(mine, jnp.concatenate([values.astype(F32), pad], axis=0).astype(BF16))
-
-    code_t, jl_t = columns(code), columns((beam & 1) * 128 + (rank & 127))
-
     def s_copy(k, d):
         return pltpu.make_async_remote_copy(
             src_ref=ret.at[k], dst_ref=retbuf.at[b], send_sem=s_send.at[k * SHARES + d], recv_sem=s_recv.at[b],
             device_id={"blk": source_of(k), "hid": d}, device_id_type=MESH,
         )
 
-    def gather(k):
-        digits = reqbuf[k]
-        low, rest = digits[0:4], digits[4:8] + 192.0
-        high = jnp.where(rest >= 96.0, 1.0, 0.0) + jnp.where(rest >= 192.0, 1.0, 0.0) + jnp.where(rest >= 288.0, 1.0, 0.0)
-        asking = rest - 96.0 * high
-        wanted = low + 256.0 * high
-        asking = jnp.concatenate([asking[r : r + 1] for r in range(ROWS)], axis=1)
-        wanted = jnp.concatenate([wanted[r : r + 1] for r in range(ROWS)], axis=1)
+    def gather(places):
+        asking, wanted = [], []
+        for u, k in enumerate(places):
+            digits = reqbuf[k].astype(F32)
+            low, rest = digits[0:4], digits[4:8] + 192.0
+            high = sum(jnp.where(rest >= 96.0 * n, 1.0, 0.0) for n in (1, 2, 3))
+            rest = rest + (Q * u - 96.0 * high)
+            low = low + 256.0 * high
+            asking += [rest[r : r + 1] for r in range(ROWS)]
+            wanted += [low[r : r + 1] for r in range(ROWS)]
+        asking, wanted = jnp.concatenate(asking, axis=1), jnp.concatenate(wanted, axis=1)
         hot = jnp.concatenate([one_hot(wanted - 256.0 * c, 256) for c in range(PARENTS // 256)], axis=0)
         found = nn(tt[...], hot)
-        query = nn(nt(eye(D), qbuf[k]).astype(BF16), one_hot(asking, Q))
-        return found, query
+        queries = nt(eye(D), jnp.concatenate([qbuf[k] for k in places], axis=0)).astype(BF16)
+        return found, nn(queries, one_hot(asking, Q * len(places)))
 
     def score(found, query):
-        bias = jnp.concatenate([bi_s[...]] * ROWS, axis=1)
-        weight = jnp.concatenate([wo_s[...]] * ROWS, axis=1)
+        width = found.shape[1] // 128
+        bias = jnp.concatenate([bi_s[...]] * width, axis=1)
+        weight = jnp.concatenate([wo_s[...]] * width, axis=1)
         shared = nn(w_all[:, 2 * D : 3 * D], query.astype(BF16)) + bias
-        rows = []
+        totals = []
         for child in range(2):
             node = found[child * D : (child + 1) * D]
             joined = jnp.concatenate([node.astype(BF16), (node * query).astype(BF16)], axis=0)
             hidden = jnp.maximum(nn(w_all[:, : 2 * D], joined) + shared, 0.0)
-            total = jnp.sum(hidden * weight, axis=0, keepdims=True)
-            rows += [total[:, r * 128 : (r + 1) * 128] for r in range(ROWS)] + [jnp.zeros((1, 128), F32)]
-        return jnp.concatenate(rows, axis=0)
+            totals.append(jnp.sum(hidden * weight, axis=0, keepdims=True))
+        scores = []
+        for u in range(width // ROWS):
+            rows = []
+            for total in totals:
+                rows += [total[:, r * 128 : (r + 1) * 128] for r in range(u * ROWS, (u + 1) * ROWS)]
+                rows += [jnp.zeros((1, 128), F32)]
+            scores.append(jnp.concatenate(rows, axis=0))
+        return scores
 
     def near(n):
         a = lax.rem(y // 2 + n // 4, 2)
@@ -267,7 +271,7 @@
                 src_ref=req.at[k], dst_ref=reqbuf.at[k], send_sem=r_send.at[k], recv_sem=r_recv.at[k],
                 device_id={"blk": source_of(k), "hid": (h + 1) % SHARES}, device_id_type=MESH,
             ).wait_recv()
-        gathered = [gather(k) for k in places]
+        found, query = gather(places)
 
         @pl.when(pair == 0)
         def _():
@@ -276,8 +280,8 @@
             bi_s[...] = jnp.broadcast_to(w_all[:, 3 * D : 3 * D + 1].astype(F32), (HID, 128))
             wo_s[...] = jnp.broadcast_to(w_all[:, 3 * D + 64 : 3 * D + 65].astype(F32), (HID, 128))
 
-        for k, (found, query) in zip(places, gathered):
-            ret[k] = score(found, query)
+        for k, scores in zip(places, score(found, query)):
+            ret[k] = scores
         for k in places:
             for d in range(SHARES):
                 here = (d == h) & (source_of(k) == b)
@@ -290,6 +294,30 @@
                 def _():
                     s_copy(k, d).start()
 
+    def all_owners(g, acc):
+        return acc + list_starts(owner, even, [g * SERVED + i for i in range(SERVED)])
+
+    rank = lax.fori_loop(0, GROUPS // SERVED, all_owners, inner[...], unroll=False)
+    code = owner * 4 + (rank >> 7)
+    mine = flag(iota((COLS, BEAM), 1) == iota((COLS, BEAM), 0) + h * COLS)
+    pad = jnp.zeros((BEAM - Q, BEAM), F32)
+
+    def columns(values):
+        return nt(mine, jnp.concatenate([values.astype(F32), pad], axis=0).astype(BF16))
+
+    code_t, jl_t = columns(code), columns((beam & 1) * 128 + (rank & 127))
+
+    @pl.loop(0, SERVED)
+    def _(i):
+        q_copy(i).wait_send()
+        r_copy(i).wait_send()
+        for d in range(SHARES):
+            @pl.when(jnp.logical_not((d == h) & (source_of(i) == b)))
+            def _():
+                s_copy(i, d).wait_send()
+
+    for d in range(1, SHARES):
+        w_copy(d).wait_send()
     @pl.loop(0, GROUPS)
     def _(o):
         @pl.when(jnp.logical_not(served_self & (o == b)))
@@ -313,18 +341,6 @@
         total = jnp.sum(jnp.where(slot_row == which, seen, 0.0), axis=0, keepdims=True)
         out_ref[c : c + 1, :] = total[:, :Q]
         out_ref[c + 1 : c + 2, :] = total[:, 128 : 128 + Q]
-
-    @pl.loop(0, SERVED)
-    def _(i):
-        q_copy(i).wait_send()
-        r_copy(i).wait_send()
-        for d in range(SHARES):
-            @pl.when(jnp.logical_not((d == h) & (source_of(i) == b)))
-            def _():
-                s_copy(i, d).wait_send()
-
-    for d in range(1, SHARES):
-        w_copy(d).wait_send()
 
 
 def shards(queries, node_table, beam, w_query, w_node, w_cross, bias_hidden, w_out):
@@ -343,8 +359,8 @@
             pltpu.VMEM((1, HID_DEV), BF16),
             pltpu.VMEM((HID, 4 * D), BF16),
             pltpu.VMEM((SERVED, Q, D), BF16),
-            pltpu.VMEM((SERVED, 8, 128), F32),
-            pltpu.VMEM((SERVED, 8, 128), F32),
+            pltpu.VMEM((SERVED, 8, 128), BF16),
+            pltpu.VMEM((SERVED, 8, 128), BF16),
             pltpu.VMEM((SERVED, 8, 128), F32),
             pltpu.VMEM((GROUPS, 8, 128), F32),
             pltpu.VMEM((2 * D, PARENTS), BF16),

time: 32.3 us -> 29.1 us (0.901)
  Pallas kernels: 30.8 us -> 27.6 us
    pallas_call x1, Pallas kernels: 30.8 us -> 27.6 us  [shards(): pl.pallas_call(kernel, out_shape=jax.ShapeDtypeStruct((COLS, Q), F32), in...]
where the time goes in v4:
time: 29.1 us; the launch traced here: 28.9 us
  Pallas kernels  27.6 us (95%)
  local copies, waits for them, and re-layouts  1.32 us (5%)
    pallas_call x1, Pallas kernels, shards(): pl.pallas_call(kernel, out_shape=jax.ShapeDtypeStruct((COLS, Q), F32), in...  27.6 us
    unnamed x1, local copies, waits for them, and re-layouts  1.32 us

profile of v4, /device:TPU:1, one launch (start us, length us, event | category | flops | bytes accessed | tf_op | source)
XLA Modules:
  0.0 28.9 jit_solution(15936103280292339722)
XLA Ops:
  0.0 27.6 %beam_scores.1 = f32[32,96]{1,0:T(8,128)} custom-call(bf16[96,128]{1,0:T(8,128)(2,1)} %q_hbm.1, bf16[2048,128]{1,0:T(8,128)(2,1)} %table_hbm.1, s32[96,128]{1,0:T(8,128)} %beam_hbm.1, bf16[64,128]{1,0:T(8,128)(2,1)} %bitcast.7, bf16[64,128]{1,0:T(8,128)(2,1)} %bitcast.8, bf16[64,128]{1,0:T(8,128)(2,1)} %bitcast.9, bf16[1,64]{1,0:T(2,128)(2,1)} %bitcast.10, ...), custom_call_target="tpu_custom_call" | custom-call | tf_op jit(solution)/shard_map/beam_scores/pallas_call | solution.py:348
  27.6 1.3 %copy.10 = f32[96,32]{0,1:T(8,128)} copy(f32[96,32]{0,1:T(8,128)} %bitcast.6) | data formatting | bytes 24576

commit v5 on v4

--- a/solution.py
+++ b/solution.py
@@ -154,21 +154,27 @@
 
     pl.semaphore_wait(barrier, SERVED + SHARES - 1)
 
+    def all_of(ref, send_sem, recv_sem):
+        return pltpu.make_async_remote_copy(
+            src_ref=ref, dst_ref=ref, send_sem=send_sem, recv_sem=recv_sem,
+            device_id={"blk": b, "hid": (h + 1) % SHARES}, device_id_type=MESH,
+        )
+
     def q_copy(i):
         return pltpu.make_async_remote_copy(
-            src_ref=q_ref, dst_ref=qbuf.at[my_place], send_sem=q_send.at[i], recv_sem=q_recv.at[my_place],
+            src_ref=q_ref, dst_ref=qbuf.at[my_place], send_sem=q_send, recv_sem=q_recv.at[my_place],
             device_id={"blk": owner_of(i), "hid": server_of(i)}, device_id_type=MESH,
         )
 
     def r_copy(i):
         return pltpu.make_async_remote_copy(
-            src_ref=req.at[i], dst_ref=reqbuf.at[my_place], send_sem=r_send.at[i], recv_sem=r_recv.at[my_place],
+            src_ref=req.at[i], dst_ref=reqbuf.at[my_place], send_sem=r_send, recv_sem=r_recv.at[my_place],
             device_id={"blk": owner_of(i), "hid": server_of(i)}, device_id_type=MESH,
         )
 
     def w_copy(d):
         return pltpu.make_async_remote_copy(
-            src_ref=w_all.at[my_rows], dst_ref=w_all.at[my_rows], send_sem=w_send.at[d - 1], recv_sem=w_recv.at[d - 1],
+            src_ref=w_all.at[my_rows], dst_ref=w_all.at[my_rows], send_sem=w_send, recv_sem=w_recv,
             device_id={"blk": b, "hid": (h + d) % SHARES}, device_id_type=MESH,
         )
 
@@ -214,7 +220,7 @@
 
     def s_copy(k, d):
         return pltpu.make_async_remote_copy(
-            src_ref=ret.at[k], dst_ref=retbuf.at[b], send_sem=s_send.at[k * SHARES + d], recv_sem=s_recv.at[b],
+            src_ref=ret.at[k], dst_ref=retbuf.at[b], send_sem=s_send, recv_sem=s_recv,
             device_id={"blk": source_of(k), "hid": d}, device_id_type=MESH,
         )
 
@@ -264,19 +270,18 @@
         places = [near(PAIR * pair + u) for u in range(PAIR)]
         for k in places:
             pltpu.make_async_remote_copy(
-                src_ref=q_ref, dst_ref=qbuf.at[k], send_sem=q_send.at[k], recv_sem=q_recv.at[k],
+                src_ref=q_ref, dst_ref=qbuf.at[k], send_sem=q_send, recv_sem=q_recv.at[k],
                 device_id={"blk": source_of(k), "hid": (h + 1) % SHARES}, device_id_type=MESH,
             ).wait_recv()
             pltpu.make_async_remote_copy(
-                src_ref=req.at[k], dst_ref=reqbuf.at[k], send_sem=r_send.at[k], recv_sem=r_recv.at[k],
+                src_ref=req.at[k], dst_ref=reqbuf.at[k], send_sem=r_send, recv_sem=r_recv.at[k],
                 device_id={"blk": source_of(k), "hid": (h + 1) % SHARES}, device_id_type=MESH,
             ).wait_recv()
         found, query = gather(places)
 
         @pl.when(pair == 0)
         def _():
-            for d in range(1, SHARES):
-                w_copy(d).wait_recv()
+            all_of(w_all.at[: HID - HID_DEV], w_send, w_recv).wait_recv()
             bi_s[...] = jnp.broadcast_to(w_all[:, 3 * D : 3 * D + 1].astype(F32), (HID, 128))
             wo_s[...] = jnp.broadcast_to(w_all[:, 3 * D + 64 : 3 * D + 65].astype(F32), (HID, 128))
 
@@ -307,25 +312,25 @@
 
     code_t, jl_t = columns(code), columns((beam & 1) * 128 + (rank & 127))
 
-    @pl.loop(0, SERVED)
-    def _(i):
-        q_copy(i).wait_send()
-        r_copy(i).wait_send()
-        for d in range(SHARES):
-            @pl.when(jnp.logical_not((d == h) & (source_of(i) == b)))
-            def _():
-                s_copy(i, d).wait_send()
-
-    for d in range(1, SHARES):
-        w_copy(d).wait_send()
-    @pl.loop(0, GROUPS)
-    def _(o):
-        @pl.when(jnp.logical_not(served_self & (o == b)))
-        def _():
-            pltpu.make_async_remote_copy(
-                src_ref=ret.at[0], dst_ref=retbuf.at[o], send_sem=s_send.at[0], recv_sem=s_recv.at[o],
-                device_id={"blk": b, "hid": (h + 1) % SHARES}, device_id_type=MESH,
-            ).wait_recv()
+    all_of(qbuf, q_send, q_recv.at[0]).wait_send()
+    all_of(reqbuf, r_send, r_recv.at[0]).wait_send()
+    all_of(w_all.at[: HID - HID_DEV], w_send, w_recv).wait_send()
+
+    @pl.when(served_self)
+    def _():
+        all_of(retbuf.at[: GROUPS - 1], s_send, s_recv).wait_send()
+
+    @pl.when(jnp.logical_not(served_self))
+    def _():
+        all_of(retbuf, s_send, s_recv).wait_send()
+
+    @pl.when(served_self)
+    def _():
+        all_of(retbuf.at[: GROUPS - 1], s_send, s_recv).wait_recv()
+
+    @pl.when(jnp.logical_not(served_self))
+    def _():
+        all_of(retbuf, s_send, s_recv).wait_recv()
 
     table = jnp.concatenate(
         [retbuf[:, 4 * child : 4 * child + 4, :].reshape(GROUPS * 4, 128) for child in range(2)], axis=1
@@ -373,15 +378,14 @@
             pltpu.VMEM((Q, BEAM), F32),
             pltpu.VMEM((HID, 128), F32),
             pltpu.VMEM((HID, 128), F32),
-            dma((8,)), dma((SERVED,)), dma((SERVED,)), dma((SERVED,)), dma((SERVED,)),
-            dma((SHARES - 1,)), dma((SHARES - 1,)), dma((SERVED * SHARES,)), dma((GROUPS,)),
+            dma((8,)), dma(()), dma((SERVED,)), dma(()), dma((SERVED,)), dma(()), dma(()), dma(()), dma(()),
         ],
-        compiler_params=pltpu.CompilerParams(collective_id=0, has_side_effects=True),
+        compiler_params=pltpu.CompilerParams(collective_id=0, has_side_effects=True, vmem_limit_bytes=16 << 20),
         name="beam_scores",
-    )(
+    )(*[pltpu.with_memory_space_constraint(x, pltpu.HBM) for x in (
         queries, node_table, beam, w_query.T, w_node.T, w_cross.T,
         bias_hidden.reshape(1, HID_DEV), w_out.reshape(1, HID_DEV),
-    )
+    )])
     return scores.T
 
 

time: 29.1 us -> 27 us (0.928)
  Pallas kernels: 27.6 us -> 26.2 us
  local copies, waits for them, and re-layouts: 1.32 us -> 0.61 us
    pallas_call x1, Pallas kernels: 27.6 us -> 26.2 us  [shards(): pl.pallas_call(kernel, out_shape=jax.ShapeDtypeStruct((COLS, Q), F32), in...]
    unnamed x1, local copies, waits for them, and re-layouts: 1.32 us -> 0.61 us
where the time goes in v5:
time: 27 us; the launch traced here: 26.8 us
  Pallas kernels  26.2 us (97%)
  local copies, waits for them, and re-layouts  0.61 us (2%)
    pallas_call x1, Pallas kernels, shards(): pl.pallas_call(kernel, out_shape=jax.ShapeDtypeStruct((COLS, Q), F32), in...  26.2 us
    unnamed x1, local copies, waits for them, and re-layouts  0.61 us

profile of v5, /device:TPU:1, one launch (start us, length us, event | category | flops | bytes accessed | tf_op | source)
XLA Modules:
  0.0 26.8 jit_solution(11352982792713249613)
XLA Ops:
  0.0 26.2 %beam_scores.1 = f32[32,96]{1,0:T(8,128)S(1)} custom-call(bf16[96,128]{1,0:T(8,128)(2,1)} %q_hbm.1, bf16[2048,128]{1,0:T(8,128)(2,1)} %table_hbm.1, s32[96,128]{1,0:T(8,128)} %beam_hbm.1, bf16[64,128]{1,0:T(8,128)(2,1)} %bitcast.7, bf16[64,128]{1,0:T(8,128)(2,1)} %bitcast.8, bf16[64,128]{1,0:T(8,128)(2,1)} %bitcast.9, bf16[1,64]{1,0:T(2,128)(2,1)} %bitcast.10, ...), custom_call_target="tpu_custom_call" | custom-call | tf_op jit(solution)/shard_map/beam_scores/pallas_call | solution.py:353
  26.2 0.6 %copy.10 = f32[96,32]{0,1:T(8,128)} copy(f32[96,32]{0,1:T(8,128)S(1)} %bitcast.6) | data formatting | bytes 24576

commit v6 on v5

--- a/solution.py
+++ b/solution.py
@@ -74,7 +74,7 @@
 def kernel(
     q_hbm, table_hbm, beam_hbm, wq_hbm, wn_hbm, wc_hbm, bias_hbm, wout_hbm, out_ref,
     q_ref, table_ref, beam_ref, w_in, bias_in, wout_in,
-    w_all, qbuf, req, reqbuf, ret, retbuf, tt, t32, keys, inner, code_s, jl_s, a_s, b_s, wo_s, bi_s,
+    w_all, qbuf, req, reqbuf, ret, retbuf, tt, t32, keys, inner, code_s, jl_s, a_s, b_s, wo_s, joined,
     in_sem, q_send, q_recv, r_send, r_recv, w_send, w_recv, s_send, s_recv,
 ):
     b, h = lax.axis_index("blk"), lax.axis_index("hid")
@@ -152,42 +152,6 @@
         w_all[my_rows, n * D : (n + 1) * D] = w_in[n]
     w_all[my_rows, 3 * D :] = nt(ident, vectors).astype(BF16)
 
-    pl.semaphore_wait(barrier, SERVED + SHARES - 1)
-
-    def all_of(ref, send_sem, recv_sem):
-        return pltpu.make_async_remote_copy(
-            src_ref=ref, dst_ref=ref, send_sem=send_sem, recv_sem=recv_sem,
-            device_id={"blk": b, "hid": (h + 1) % SHARES}, device_id_type=MESH,
-        )
-
-    def q_copy(i):
-        return pltpu.make_async_remote_copy(
-            src_ref=q_ref, dst_ref=qbuf.at[my_place], send_sem=q_send, recv_sem=q_recv.at[my_place],
-            device_id={"blk": owner_of(i), "hid": server_of(i)}, device_id_type=MESH,
-        )
-
-    def r_copy(i):
-        return pltpu.make_async_remote_copy(
-            src_ref=req.at[i], dst_ref=reqbuf.at[my_place], send_sem=r_send, recv_sem=r_recv.at[my_place],
-            device_id={"blk": owner_of(i), "hid": server_of(i)}, device_id_type=MESH,
-        )
-
-    def w_copy(d):
-        return pltpu.make_async_remote_copy(
-            src_ref=w_all.at[my_rows], dst_ref=w_all.at[my_rows], send_sem=w_send, recv_sem=w_recv,
-            device_id={"blk": b, "hid": (h + d) % SHARES}, device_id_type=MESH,
-        )
-
-    for d in range(1, SHARES):
-        w_copy(d).start()
-
-    def far(n):
-        return lax.rem(y + 2 + n // 2, 4) * 2 + lax.rem(z // 2 + 1 + n, 2)
-
-    @pl.loop(0, SERVED)
-    def _(n):
-        q_copy(far(n)).start()
-
     row64 = iota((64, BEAM), 0)
     target = ((row64 >> 3) * 4 + (row64 & 3)).astype(F32).astype(BF16)
     is_b = ((iota((16, BEAM), 0) >> 2) & 1).astype(F32).astype(BF16)
@@ -207,9 +171,42 @@
     for i in range(SERVED):
         req[i] = tables[8 * i : 8 * i + 8].astype(BF16)
 
+    pl.semaphore_wait(barrier, SERVED + SHARES - 1)
+
+    def all_of(ref, send_sem, recv_sem):
+        return pltpu.make_async_remote_copy(
+            src_ref=ref, dst_ref=ref, send_sem=send_sem, recv_sem=recv_sem,
+            device_id={"blk": b, "hid": (h + 1) % SHARES}, device_id_type=MESH,
+        )
+
+    def q_copy(i):
+        return pltpu.make_async_remote_copy(
+            src_ref=q_ref, dst_ref=qbuf.at[my_place], send_sem=q_send, recv_sem=q_recv.at[my_place],
+            device_id={"blk": owner_of(i), "hid": server_of(i)}, device_id_type=MESH,
+        )
+
+    def r_copy(i):
+        return pltpu.make_async_remote_copy(
+            src_ref=req.at[i], dst_ref=reqbuf.at[my_place], send_sem=r_send, recv_sem=r_recv.at[my_place],
+            device_id={"blk": owner_of(i), "hid": server_of(i)}, device_id_type=MESH,
+        )
+
+    def w_copy(d):
+        return pltpu.make_async_remote_copy(
+            src_ref=w_all.at[my_rows], dst_ref=w_all.at[my_rows], send_sem=w_send, recv_sem=w_recv,
+            device_id={"blk": b, "hid": (h + d) % SHARES}, device_id_type=MESH,
+        )
+
+    for d in range(1, SHARES):
+        w_copy(d).start()
+
+    def far(n):
+        return lax.rem(y + 2 + n // 2, 4) * 2 + lax.rem(z // 2 + 1 + n, 2)
+
     @pl.loop(0, SERVED)
     def _(n):
         r_copy(far(n)).start()
+        q_copy(far(n)).start()
 
     loads[7].wait()
     t32[...] = table_ref[...].astype(F32)
@@ -218,13 +215,17 @@
         half = t32[pl.ds(child, PARENTS, stride=2), :].astype(BF16)
         tt[child * D : (child + 1) * D, :] = nt(ident, half).astype(BF16)
 
+    one_row = flag(iota((D, PAIR * SLOTS), 0) == 0)
+    for slot in range(2):
+        joined[slot, 5 * D :] = one_row
+
     def s_copy(k, d):
         return pltpu.make_async_remote_copy(
             src_ref=ret.at[k], dst_ref=retbuf.at[b], send_sem=s_send, recv_sem=s_recv,
             device_id={"blk": source_of(k), "hid": d}, device_id_type=MESH,
         )
 
-    def gather(places):
+    def gather(places, slot):
         asking, wanted = [], []
         for u, k in enumerate(places):
             digits = reqbuf[k].astype(F32)
@@ -238,18 +239,20 @@
         hot = jnp.concatenate([one_hot(wanted - 256.0 * c, 256) for c in range(PARENTS // 256)], axis=0)
         found = nn(tt[...], hot)
         queries = nt(eye(D), jnp.concatenate([qbuf[k] for k in places], axis=0)).astype(BF16)
-        return found, nn(queries, one_hot(asking, Q * len(places)))
-
-    def score(found, query):
-        width = found.shape[1] // 128
-        bias = jnp.concatenate([bi_s[...]] * width, axis=1)
+        query = nn(queries, one_hot(asking, Q * len(places)))
+        for child in range(2):
+            node = found[child * D : (child + 1) * D]
+            joined[slot, 2 * child * D : (2 * child + 1) * D] = node.astype(BF16)
+            joined[slot, (2 * child + 1) * D : (2 * child + 2) * D] = (node * query).astype(BF16)
+        joined[slot, 4 * D : 5 * D] = query.astype(BF16)
+
+    def score(slot):
+        width = joined.shape[2] // 128
         weight = jnp.concatenate([wo_s[...]] * width, axis=1)
-        shared = nn(w_all[:, 2 * D : 3 * D], query.astype(BF16)) + bias
+        shared = nn(w_all[:, 2 * D :], joined[slot, 4 * D : 6 * D])
         totals = []
         for child in range(2):
-            node = found[child * D : (child + 1) * D]
-            joined = jnp.concatenate([node.astype(BF16), (node * query).astype(BF16)], axis=0)
-            hidden = jnp.maximum(nn(w_all[:, : 2 * D], joined) + shared, 0.0)
+            hidden = jnp.maximum(nn(w_all[:, : 2 * D], joined[slot, 2 * child * D : 2 * (child + 1) * D]) + shared, 0.0)
             totals.append(jnp.sum(hidden * weight, axis=0, keepdims=True))
         scores = []
         for u in range(width // ROWS):
@@ -265,9 +268,7 @@
         e = lax.rem(xh + n, 2)
         return a * 4 + e * 2 + lax.rem(z // 2 + n // 2, 2)
 
-    @pl.loop(0, SERVED // PAIR)
-    def _(pair):
-        places = [near(PAIR * pair + u) for u in range(PAIR)]
+    def arrive(places):
         for k in places:
             pltpu.make_async_remote_copy(
                 src_ref=q_ref, dst_ref=qbuf.at[k], send_sem=q_send, recv_sem=q_recv.at[k],
@@ -277,16 +278,19 @@
                 src_ref=req.at[k], dst_ref=reqbuf.at[k], send_sem=r_send, recv_sem=r_recv.at[k],
                 device_id={"blk": source_of(k), "hid": (h + 1) % SHARES}, device_id_type=MESH,
             ).wait_recv()
-        found, query = gather(places)
-
-        @pl.when(pair == 0)
-        def _():
-            all_of(w_all.at[: HID - HID_DEV], w_send, w_recv).wait_recv()
-            bi_s[...] = jnp.broadcast_to(w_all[:, 3 * D : 3 * D + 1].astype(F32), (HID, 128))
-            wo_s[...] = jnp.broadcast_to(w_all[:, 3 * D + 64 : 3 * D + 65].astype(F32), (HID, 128))
-
-        for k, scores in zip(places, score(found, query)):
+
+    steps = [[near(PAIR * pair + u) for u in range(PAIR)] for pair in range(SERVED // PAIR)]
+    arrive(steps[0])
+    gather(steps[0], 0)
+    all_of(w_all.at[: HID - HID_DEV], w_send, w_recv).wait_recv()
+    wo_s[...] = jnp.broadcast_to(w_all[:, 3 * D + 64 : 3 * D + 65].astype(F32), (HID, 128))
+    for pair, places in enumerate(steps):
+        if pair + 1 < len(steps):
+            arrive(steps[pair + 1])
+        for k, scores in zip(places, score(pair % 2)):
             ret[k] = scores
+        if pair + 1 < len(steps):
+            gather(steps[pair + 1], (pair + 1) % 2)
         for k in places:
             for d in range(SHARES):
                 here = (d == h) & (source_of(k) == b)
@@ -377,7 +381,7 @@
             pltpu.VMEM((Q, BEAM), F32),
             pltpu.VMEM((Q, BEAM), F32),
             pltpu.VMEM((HID, 128), F32),
-            pltpu.VMEM((HID, 128), F32),
+            pltpu.VMEM((2, 6 * D, PAIR * SLOTS), BF16),
             dma((8,)), dma(()), dma((SERVED,)), dma(()), dma((SERVED,)), dma(()), dma(()), dma(()), dma(()),
         ],
         compiler_params=pltpu.CompilerParams(collective_id=0, has_side_effects=True, vmem_limit_bytes=16 << 20),

time: 27 us -> 26.6 us (0.985)
  Pallas kernels: 26.2 us -> 25.9 us
    pallas_call x1, Pallas kernels: 26.2 us -> 25.9 us  [shards(): pl.pallas_call(kernel, out_shape=jax.ShapeDtypeStruct((COLS, Q), F32), in...]
where the time goes in v6:
time: 26.6 us; the launch traced here: 26.5 us
  Pallas kernels  25.9 us (97%)
  local copies, waits for them, and re-layouts  0.61 us (2%)
    pallas_call x1, Pallas kernels, shards(): pl.pallas_call(kernel, out_shape=jax.ShapeDtypeStruct((COLS, Q), F32), in...  25.9 us
    unnamed x1, local copies, waits for them, and re-layouts  0.61 us

profile of v6, /device:TPU:1, one launch (start us, length us, event | category | flops | bytes accessed | tf_op | source)
XLA Modules:
  0.0 26.5 jit_solution(3729924644433369973)
XLA Ops:
  0.0 25.9 %beam_scores.1 = f32[32,96]{1,0:T(8,128)S(1)} custom-call(bf16[96,128]{1,0:T(8,128)(2,1)} %q_hbm.1, bf16[2048,128]{1,0:T(8,128)(2,1)} %table_hbm.1, s32[96,128]{1,0:T(8,128)} %beam_hbm.1, bf16[64,128]{1,0:T(8,128)(2,1)} %bitcast.7, bf16[64,128]{1,0:T(8,128)(2,1)} %bitcast.8, bf16[64,128]{1,0:T(8,128)(2,1)} %bitcast.9, bf16[1,64]{1,0:T(2,128)(2,1)} %bitcast.10, ...), custom_call_target="tpu_custom_call" | custom-call | tf_op jit(solution)/shard_map/beam_scores/pallas_call | solution.py:357
  25.9 0.6 %copy.10 = f32[96,32]{0,1:T(8,128)} copy(f32[96,32]{0,1:T(8,128)S(1)} %bitcast.6) | data formatting | bytes 24576

commit v7 on v6

--- a/solution.py
+++ b/solution.py
@@ -288,7 +288,7 @@
         if pair + 1 < len(steps):
             arrive(steps[pair + 1])
         for k, scores in zip(places, score(pair % 2)):
-            ret[k] = scores
+            ret[k] = scores.astype(BF16)
         if pair + 1 < len(steps):
             gather(steps[pair + 1], (pair + 1) % 2)
         for k in places:
@@ -336,17 +336,15 @@
     def _():
         all_of(retbuf, s_send, s_recv).wait_recv()
 
+    table = retbuf[...].astype(F32)
     table = jnp.concatenate(
-        [retbuf[:, 4 * child : 4 * child + 4, :].reshape(GROUPS * 4, 128) for child in range(2)], axis=1
-    )
-    coarse = table.astype(BF16)
-    parts = jnp.concatenate([coarse, (table - coarse.astype(F32)).astype(BF16)], axis=0)
+        [table[:, 4 * child : 4 * child + 4, :].reshape(GROUPS * 4, 128) for child in range(2)], axis=1
+    ).astype(BF16)
     slot_row = iota((GROUPS * 4, 2 * 128), 0).astype(F32)
     for c in range(0, COLS, 2):
         hot = one_hot(jnp.concatenate([jl_t[c : c + 1], jl_t[c + 1 : c + 2]], axis=1), 256)
         which = jnp.concatenate([code_t[c : c + 1], code_t[c + 1 : c + 2]], axis=1)
-        seen = nn(parts, hot)
-        seen = seen[: GROUPS * 4] + seen[GROUPS * 4 :]
+        seen = nn(table, hot)
         total = jnp.sum(jnp.where(slot_row == which, seen, 0.0), axis=0, keepdims=True)
         out_ref[c : c + 1, :] = total[:, :Q]
         out_ref[c + 1 : c + 2, :] = total[:, 128 : 128 + Q]
@@ -370,8 +368,8 @@
             pltpu.VMEM((SERVED, Q, D), BF16),
             pltpu.VMEM((SERVED, 8, 128), BF16),
             pltpu.VMEM((SERVED, 8, 128), BF16),
-            pltpu.VMEM((SERVED, 8, 128), F32),
-            pltpu.VMEM((GROUPS, 8, 128), F32),
+            pltpu.VMEM((SERVED, 8, 128), BF16),
+            pltpu.VMEM((GROUPS, 8, 128), BF16),
             pltpu.VMEM((2 * D, PARENTS), BF16),
             pltpu.VMEM((2 * PARENTS, D), F32),
             pltpu.VMEM((BEAM, BEAM), I32),

time: 26.6 us -> 26.3 us (0.989)
  Pallas kernels: 25.9 us -> 25.6 us
    pallas_call x1, Pallas kernels: 25.9 us -> 25.6 us  [shards(): pl.pallas_call(kernel, out_shape=jax.ShapeDtypeStruct((COLS, Q), F32), in...]
where the time goes in v7:
time: 26.3 us; the launch traced here: 26.2 us
  Pallas kernels  25.6 us (97%)
  local copies, waits for them, and re-layouts  0.61 us (2%)
    pallas_call x1, Pallas kernels, shards(): pl.pallas_call(kernel, out_shape=jax.ShapeDtypeStruct((COLS, Q), F32), in...  25.6 us
    unnamed x1, local copies, waits for them, and re-layouts  0.61 us

profile of v7, /device:TPU:1, one launch (start us, length us, event | category | flops | bytes accessed | tf_op | source)
XLA Modules:
  0.0 26.2 jit_solution(5127439252598164169)
XLA Ops:
  0.0 25.6 %beam_scores.1 = f32[32,96]{1,0:T(8,128)S(1)} custom-call(bf16[96,128]{1,0:T(8,128)(2,1)} %q_hbm.1, bf16[2048,128]{1,0:T(8,128)(2,1)} %table_hbm.1, s32[96,128]{1,0:T(8,128)} %beam_hbm.1, bf16[64,128]{1,0:T(8,128)(2,1)} %bitcast.7, bf16[64,128]{1,0:T(8,128)(2,1)} %bitcast.8, bf16[64,128]{1,0:T(8,128)(2,1)} %bitcast.9, bf16[1,64]{1,0:T(2,128)(2,1)} %bitcast.10, ...), custom_call_target="tpu_custom_call" | custom-call | tf_op jit(solution)/shard_map/beam_scores/pallas_call | solution.py:355
  25.6 0.6 %copy.10 = f32[96,32]{0,1:T(8,128)} copy(f32[96,32]{0,1:T(8,128)S(1)} %bitcast.6) | data formatting | bytes 24576

commit v8 on v7

--- a/solution.py
+++ b/solution.py
@@ -200,13 +200,13 @@
     for d in range(1, SHARES):
         w_copy(d).start()
 
-    def far(n):
-        return lax.rem(y + 2 + n // 2, 4) * 2 + lax.rem(z // 2 + 1 + n, 2)
+    def ahead(n):
+        return lax.rem(y + n // 2, 4) * 2 + lax.rem(z // 2 + n, 2)
 
     @pl.loop(0, SERVED)
     def _(n):
-        r_copy(far(n)).start()
-        q_copy(far(n)).start()
+        r_copy(ahead(n)).start()
+        q_copy(ahead(n)).start()
 
     loads[7].wait()
     t32[...] = table_ref[...].astype(F32)

time: 26.3 us -> 25.8 us (0.981)
  Pallas kernels: 25.6 us -> 25.1 us
    pallas_call x1, Pallas kernels: 25.6 us -> 25.1 us  [shards(): pl.pallas_call(kernel, out_shape=jax.ShapeDtypeStruct((COLS, Q), F32), in...]
where the time goes in v8:
time: 25.8 us; the launch traced here: 25.7 us
  Pallas kernels  25.1 us (97%)
  local copies, waits for them, and re-layouts  0.61 us (2%)
    pallas_call x1, Pallas kernels, shards(): pl.pallas_call(kernel, out_shape=jax.ShapeDtypeStruct((COLS, Q), F32), in...  25.1 us
    unnamed x1, local copies, waits for them, and re-layouts  0.61 us

profile of v8, /device:TPU:1, one launch (start us, length us, event | category | flops | bytes accessed | tf_op | source)
XLA Modules:
  0.0 25.7 jit_solution(9011670550645575037)
XLA Ops:
  0.0 25.1 %beam_scores.1 = f32[32,96]{1,0:T(8,128)S(1)} custom-call(bf16[96,128]{1,0:T(8,128)(2,1)} %q_hbm.1, bf16[2048,128]{1,0:T(8,128)(2,1)} %table_hbm.1, s32[96,128]{1,0:T(8,128)} %beam_hbm.1, bf16[64,128]{1,0:T(8,128)(2,1)} %bitcast.7, bf16[64,128]{1,0:T(8,128)(2,1)} %bitcast.8, bf16[64,128]{1,0:T(8,128)(2,1)} %bitcast.9, bf16[1,64]{1,0:T(2,128)(2,1)} %bitcast.10, ...), custom_call_target="tpu_custom_call" | custom-call | tf_op jit(solution)/shard_map/beam_scores/pallas_call | solution.py:355
  25.1 0.6 %copy.10 = f32[96,32]{0,1:T(8,128)} copy(f32[96,32]{0,1:T(8,128)S(1)} %bitcast.6) | data formatting | bytes 24576
